TPU v7x, 32 devices: a whole 2x2x4 slice. The times are simulated.
32 devices in a mesh: dp: 2 (over x), tpa: 4 (over z), tpb: 4 (over y, core).
Axes of the slice: x: 2, y: 2, z: 4, core: 2. Of those that a mesh axis runs over, the one named last changes fastest.
Arguments:
- hidden: bfloat16 [512, 7, 2048], P('dp'), parts along dimension 0
- w_head: bfloat16 [2048, 49152], P(None, ('tpa', 'tpb'))
- q_draft: float32 [512, 6, 49152], P(('dp', 'tpa', 'tpb')), parts along dimension 0
- x_draft: int32 [512, 6], P('dp'), parts along dimension 0
Outputs:
- output 1: float32 [512, 6], P('dp'), parts along dimension 0
- output 2: float32 [512], P('dp'), parts along dimension 0
- output 3: float32 [512, 6, 49152], P('dp', None, ('tpa', 'tpb')), parts along dimension 0
- output 4: float32 [512, 49152], P('dp', ('tpa', 'tpb')), parts along dimension 0
There are 2 independent parts. A program takes and returns all parts, laid end to end along the dimension named above; an argument that names none is the same for every part.
All inputs are finite; a program needn't handle non-finite values.
Results may differ from a plain program's by a relative error of at most 0.001.
Values are sent between devices in bfloat16 or wider.
A program may use at most 1 GiB of HBM per device.

v0:
```python
import jax
import jax.numpy as jnp
from jax import lax
from jax.sharding import PartitionSpec as P

INV_TEMP = 1.25
VOCAB_AXES = ("tpa", "tpb")


def solution(mesh):
    tpb_size = mesh.shape["tpb"]

    def local_step(hidden, w_head, q_draft, x_draft):
        num_draft = x_draft.shape[1]
        vocab_local = w_head.shape[1]
        logits = jnp.einsum("bgd,dv->bgv", hidden, w_head, preferred_element_type=jnp.float32) * INV_TEMP
        glob_max = lax.pmax(jnp.max(logits, axis=-1), VOCAB_AXES)
        exp_vals = jnp.exp(logits - glob_max[..., None])
        exp_sum = lax.psum(jnp.sum(exp_vals, axis=-1), VOCAB_AXES)
        prob_all = exp_vals / exp_sum[..., None]
        q_vocab = lax.all_to_all(q_draft, VOCAB_AXES, 2, 0, tiled=True)
        p_draft = prob_all[:, :num_draft, :]
        shard_idx = lax.axis_index("tpa") * tpb_size + lax.axis_index("tpb")
        local_ids = x_draft - shard_idx * vocab_local
        is_owned = (local_ids >= 0) & (local_ids < vocab_local)
        safe_ids = jnp.clip(local_ids, 0, vocab_local - 1)[..., None]
        p_pick = jnp.where(is_owned, jnp.take_along_axis(p_draft, safe_ids, axis=2)[..., 0], 0.0)
        q_pick = jnp.where(is_owned, jnp.take_along_axis(q_vocab, safe_ids, axis=2)[..., 0], 0.0)
        excess = jnp.maximum(p_draft - q_vocab, 0.0)
        reduced = lax.psum(jnp.stack([p_pick, q_pick, jnp.sum(excess, axis=-1)]), VOCAB_AXES)
        accept = jnp.minimum(1.0, reduced[0] / reduced[1])
        expected = jnp.sum(jnp.cumprod(accept, axis=1), axis=1)
        residual = excess / reduced[2][..., None]
        return accept, expected, residual, prob_all[:, num_draft, :]

    return jax.shard_map(
        local_step, mesh=mesh,
        in_specs=(P("dp", None, None), P(None, VOCAB_AXES), P(("dp",) + VOCAB_AXES, None, None), P("dp", None)),
        out_specs=(P("dp", None), P("dp"), P("dp", None, VOCAB_AXES), P("dp", VOCAB_AXES)),
        check_vma=False)
```

profile of v0, /device:TPU:0, one launch (start us, length us, event | category | flops | bytes accessed | tf_op | source)
XLA Modules:
  0.0 1224.0 jit_solution(5023611428782158033)
XLA Ops:
  0.6 91.4 %copy.23 = f32[16,6,49152]{0,1,2:T(8,128)} copy(f32[16,6,49152]{2,0,1:T(8,128)} %param.8) | data formatting | bytes 37748736 | tf_op args[2]
  92.1 159.1 %reshape.62 = f32[16,1,294912]{2,1,0:T(1,128)} reshape(f32[49152,6,16]{2,1,0:T(8,128)} %bitcast.42) | data formatting | bytes 37748736
  251.1 0.0 copy-start.5
  251.1 7.6 all-to-all-start
  258.8 0.0 copy-done.5
  258.8 0.1 copy.22
  258.9 0.0 copy-start.2
  259.1 0.1 fusion.6
  259.2 0.7 reshape.51
  259.9 30.3 %multiply_reduce_fusion = (f32[256,7]{0,1:T(8,128)S(1)}, f32[256,7,3072]{2,0,1:T(8,128)}) fusion(bf16[256,7,2048]{2,0,1:T(8,128)(2,1)} %param.6, bf16[2048,3072]{1,0:T(8,128)(2,1)} %param.7), kind=kOutput, calls=%fused_computation.3 | convolution fusion | flops 22559586304 | bytes 41950208 | tf_op jit(solution)/shard_map/bgd,dv->bgv/dot_general | solution.py:16
  290.2 0.0 copy-done.2
  290.2 338.1 %pmax.7 = f32[256,7]{0,1:T(8,128)S(1)} all-reduce(f32[256,7]{0,1:T(8,128)S(1)} %get-tuple-element.16), channel_id=1, replica_groups=mesh['dp'=2,'tpa'=4,'tpb'=4] {'tpa','tpb'}, use_global_device_ids=true, to_apply=%region_1.0 | all-reduce | flops 1792 | bytes 14336 | tf_op jit(solution)/shard_map/pmax | solution.py:17
  628.4 10.1 fusion.1
  638.4 82.2 %psum.14 = f32[256,7]{0,1:T(8,128)S(1)} all-reduce(f32[256,7]{0,1:T(8,128)S(1)} %fusion.1), channel_id=1, replica_groups=mesh['dp'=2,'tpa'=4,'tpb'=4] {'tpa','tpb'}, use_global_device_ids=true, to_apply=%region_3.0 | all-reduce | flops 1792 | bytes 14336 | tf_op jit(solution)/shard_map/psum | solution.py:19
  720.6 10.0 fusion
  730.7 0.0 copy-start.1
  730.7 7.3 copy-done.1
  738.0 2.0 slice_bitcast_fusion
  740.0 0.0 all-to-all-done
  740.0 0.5 broadcast.76
  740.5 54.1 %reduce = f32[16,294912]{1,0:T(8,128)} reduce(f32[16,1,294912]{2,1,0:T(1,128)} %all-to-all-done, f32[]{:T(128)} %broadcast.76), dimensions={1}, to_apply=%all_to_all.13.reduce_sub_computation | reduce | bytes 37748740 | tf_op jit(solution)/shard_map/all_to_all | solution.py:21
  794.7 184.9 %reshape.63 = f32[49152,6,16]{2,1,0:T(8,128)} reshape(f32[16,294912]{1,0:T(8,128)} %reduce) | data formatting | bytes 37748736
  979.6 102.5 %copy.24 = f32[16,6,16,3072]{3,0,2,1:T(8,128)} copy(f32[16,6,16,3072]{0,1,3,2:T(8,128)} %bitcast.6) | data formatting | bytes 37748736 | tf_op jit(solution)/shard_map/all_to_all | solution.py:21
  1082.1 0.0 copy-start
  1082.1 18.9 %fusion.15 = (f32[256,6,3072]{2,0,1:T(8,128)}, f32[256,6]{0,1:T(8,128)S(1)}) fusion(f32[256,7,3072]{2,0,1:T(8,128)} %copy-done.1, f32[16,6,16,3072]{3,0,2,1:T(8,128)} %copy.24), kind=kLoop, calls=%fused_computation.34 | loop fusion | flops 14154240 | bytes 56629248 | tf_op jit(solution)/shard_map/slice | solution.py:22
  1100.9 0.0 copy-done
  1100.9 0.0 copy-start.3
  1100.9 21.7 %gather_fusion = f32[1536]{0:T(1024)S(1)} fusion(f32[256,6,3072]{2,0,1:T(8,128)} %get-tuple-element.12, s32[1536]{0:T(1024)S(1)} %copy-done), kind=kCustom, calls=%fused_computation.clone | custom fusion | bytes 30720 | tf_op jit(solution)/shard_map/jit(take_along_axis)/gather | solution.py:27
  1122.7 0.1 reshape.54
  1122.8 0.0 copy-done.3
  1122.8 0.1 fusion.11
  1122.9 23.0 %gather_fusion.1 = f32[1536]{0:T(1024)S(1)} fusion(f32[256,6,3072]{2,0,1:T(8,128)} %bitcast.48, s32[1536]{0:T(1024)S(1)} %copy-done), kind=kCustom, calls=%fused_computation.1.clone | custom fusion | bytes 30720 | tf_op jit(solution)/shard_map/jit(take_along_axis)/gather | solution.py:28
  1145.9 0.1 reshape.60
  1146.1 0.1 copy.26
  1146.2 0.1 copy.25
  1146.3 57.6 %psum.15 = f32[3,256,6]{1,2,0:T(8,128)S(1)} all-reduce(f32[3,256,6]{1,2,0:T(8,128)S(1)} %pad_maximum_fusion), channel_id=1, replica_groups=mesh['dp'=2,'tpa'=4,'tpb'=4] {'tpa','tpb'}, use_global_device_ids=true, to_apply=%region_5.7 | all-reduce | flops 4608 | bytes 36864 | tf_op jit(solution)/shard_map/psum | solution.py:30
  1203.9 0.0 copy-start.4
  1203.9 19.1 %broadcast_divide_fusion = f32[256,6,3072]{2,0,1:T(8,128)} fusion(f32[256,6]{0,1:T(8,128)S(1)} %get-tuple-element.14, f32[16,6,16,3072]{3,0,2,1:T(8,128)} %copy.24, f32[256,7,3072]{2,0,1:T(8,128)} %copy-done.1), kind=kLoop, calls=%fused_computation.9 | loop fusion | flops 14155776 | bytes 56629248 | tf_op jit(solution)/shard_map/div | solution.py:33
  1222.9 0.0 copy-done.4
  1223.0 0.6 reduce_sum.29
  (8 shorter events, 0.2 us)
Async XLA Ops:
  251.1 7.6 copy-start.5
  251.1 488.9 %all-to-all-start = ((f32[16,1,294912]{2,1,0:T(1,128)}), f32[16,1,294912]{2,1,0:T(1,128)}, u32[]{:S(2)}, u32[]{:S(2)}) async-start(f32[16,1,294912]{2,1,0:T(1,128)} %reshape.62), calls=%async_computation | async-start | bytes 37748736 | tf_op jit(solution)/shard_map/all_to_all | solution.py:21
  258.9 31.3 %copy-start.2 = (s32[256,6]{1,0:T(8,128)}, s32[256,6]{1,0:T(8,128)S(1)}, u32[]{:S(2)}) copy-start(s32[256,6]{1,0:T(8,128)S(1)} %copy.22) | copy-start | bytes 18436
  730.7 7.4 copy-start.1
  1082.1 18.9 %copy-start = (s32[1536]{0:T(1024)S(1)}, s32[1536]{0:T(1024)}, u32[]{:S(2)}) copy-start(s32[1536]{0:T(1024)} %reshape.51) | copy-start | bytes 18436
  1100.9 21.9 %copy-start.3 = (s32[256,6]{1,0:T(8,128)S(1)}, s32[256,6]{1,0:T(8,128)}, u32[]{:S(2)}) copy-start(s32[256,6]{1,0:T(8,128)} %copy-done.2) | copy-start | bytes 18436
  1203.9 19.1 %copy-start.4 = (f32[256,6]{0,1:T(8,128)}, f32[256,6]{0,1:T(8,128)S(1)}, u32[]{:S(2)}) copy-start(f32[256,6]{0,1:T(8,128)S(1)} %get-tuple-element.15) | copy-start | bytes 18436
where the time goes:
time: 1240 us; the launch traced here: 1220 us
  local copies, waits for them, and re-layouts  594 us (48%)
  blocking collectives  478 us (39%)
  other arithmetic  113 us (9%)
  matrix products  30.3 us (2%)
    unnamed x16, local copies, waits for them, and re-layouts  443 us
    pmax x1, blocking collectives, local_step(): glob_max = lax.pmax(jnp.max(logits, axis=-1), VOCAB_AXES)  338 us
    all_to_all x2, local copies, waits for them, and re-layouts, local_step(): q_vocab = lax.all_to_all(q_draft, VOCAB_AXES, 2, 0, tiled=True)  103 us
    psum x1, blocking collectives, local_step(): exp_sum = lax.psum(jnp.sum(exp_vals, axis=-1), VOCAB_AXES)  82.2 us
    psum x1, blocking collectives, local_step(): lax.psum(jnp.stack([p_pick, q_pick, jnp.sum(excess, axis=-1)]), VOCAB_AXES)  57.6 us
    all_to_all x1, other arithmetic, local_step(): q_vocab = lax.all_to_all(q_draft, VOCAB_AXES, 2, 0, tiled=True)  54.1 us
    dot_general x1, matrix products, local_step(): jnp.einsum('bgd,dv->bgv', hidden, w_head, preferred_element_type=jnp.floa...  30.3 us
  transfers between devices with their start and end apart: 1, of which 0 were waited for; matrix products, arithmetic and copies ran while one was open for 4% of the time, Pallas kernels for 0%

commit v1 on v0

v1 whole, which is shorter than its diff:
```python
import functools

import jax
import jax.numpy as jnp
from jax import lax
from jax.experimental import pallas as pl
from jax.experimental.pallas import tpu as pltpu
from jax.sharding import PartitionSpec as P

INV_TEMP = 1.25
VOCAB_AXES = ("tpa", "tpb")
MESH = pl.DeviceIdType.MESH
F32 = jnp.float32
FAR = ((3, 3, 0, 0), (2, 0, 3, 1), (1, 2, 1, 2))
CORE_OFFSETS = (0, 2, 1, 3)
NT = 512


def pick(index, values):
    out = jnp.int32(values[-1])
    for k in range(len(values) - 2, -1, -1):
        out = jnp.where(index == k, jnp.int32(values[k]), out)
    return out


def diag(n):
    return lax.broadcasted_iota(jnp.int32, (n, n), 0) == lax.broadcasted_iota(jnp.int32, (n, n), 1)


def to_col(row):
    return jnp.sum(jnp.where(diag(row.shape[1]), row, 0.0), axis=1, keepdims=True)


def to_row(col):
    return jnp.sum(jnp.where(diag(col.shape[0]), col, 0.0), axis=0, keepdims=True)


def put_row(acc, i, row):
    return jnp.where(lax.broadcasted_iota(jnp.int32, acc.shape, 0) == i, row, acc)


def get_row(rows, i):
    return jnp.sum(jnp.where(lax.broadcasted_iota(jnp.int32, rows.shape, 0) == i, rows, 0.0), axis=0, keepdims=True)


def exchange_kernel(dims, hid_ref, w_ref, q_ref, x_ref, ex_ref, bonus_ref, sums_ref,
                    hid_v, w_v, p_v, tok_v, stat_v, hid_sem, w_sem, own_sem,
                    q_send, q_recv, s_send, s_recv, z_send, z_recv):
    n_pos, seqs, depth, vocab, local_seqs, na, nb = dims
    n_draft = n_pos - 1
    n_peers = na * nb
    n_tiles = vocab // NT
    dp, za, tb = lax.axis_index("dp"), lax.axis_index("tpa"), lax.axis_index("tpb")
    me = za * nb + tb

    def peer(k):
        if isinstance(k, int):
            plane = pick(za, FAR[k // nb]) if k < 12 else za
            off = CORE_OFFSETS[k % nb] if k < 12 else k - 11
        else:
            group = k // nb
            plane = jnp.where(group == 0, pick(za, FAR[0]), jnp.where(group == 1, pick(za, FAR[1]),
                              jnp.where(group == 2, pick(za, FAR[2]), za)))
            off = jnp.where(k < 12, pick(lax.rem(k, nb), CORE_OFFSETS), k - 11)
        return plane, lax.rem(tb + off, nb)

    def q_copy(plane, core):
        other = plane * nb + core
        return pltpu.make_async_remote_copy(
            src_ref=q_ref.at[:, :, pl.ds(pl.multiple_of(other * vocab, 128), vocab)],
            dst_ref=ex_ref.at[:, pl.ds(pl.multiple_of(me * local_seqs, 8), local_seqs), :],
            send_sem=q_send.at[other], recv_sem=q_recv.at[me],
            device_id=(dp, plane, core), device_id_type=MESH)

    def q_arrival(other):
        return pltpu.make_async_remote_copy(
            src_ref=q_ref.at[:, :, pl.ds(0, vocab)],
            dst_ref=ex_ref.at[:, pl.ds(pl.multiple_of(other * local_seqs, 8), local_seqs), :],
            send_sem=q_send.at[other], recv_sem=q_recv.at[other],
            device_id=(dp, za, tb), device_id_type=MESH)

    def small_copy(ref, send, recv, slot, plane, core):
        other = plane * nb + core
        return pltpu.make_async_remote_copy(
            src_ref=ref.at[slot], dst_ref=ref.at[slot],
            send_sem=send.at[other], recv_sem=recv.at[slot],
            device_id=(dp, plane, core), device_id_type=MESH)

    def small_arrival(ref, send, recv, other):
        return pltpu.make_async_remote_copy(
            src_ref=ref.at[other], dst_ref=ref.at[other],
            send_sem=send.at[other], recv_sem=recv.at[other],
            device_id=(dp, za, tb), device_id_type=MESH)

    def w_copy(tile, slot):
        return pltpu.make_async_copy(w_ref.at[:, pl.ds(pl.multiple_of(tile * NT, NT), NT)], w_v.at[slot], w_sem.at[slot])

    hid_copy = pltpu.make_async_copy(hid_ref, hid_v, hid_sem)
    own_copy = pltpu.make_async_copy(
        q_ref.at[:, :, pl.ds(pl.multiple_of(me * vocab, 128), vocab)],
        ex_ref.at[:, pl.ds(pl.multiple_of(me * local_seqs, 8), local_seqs), :], own_sem)

    barrier = pltpu.get_barrier_semaphore()
    for k in range(1, n_peers):
        pl.semaphore_signal(barrier, inc=1, device_id=(dp, lax.rem(za + k // nb, na), lax.rem(tb + k % nb, nb)),
                            device_id_type=MESH)
    pl.semaphore_wait(barrier, n_peers - 1)

    for k in range(8):
        q_copy(*peer(k)).start()
    hid_copy.start()
    w_copy(0, 0).start()
    own_copy.start()

    first_id = me * vocab
    tok_rows = x_ref[...].astype(F32)
    for i in range(n_draft):
        tok_v[i] = jnp.broadcast_to(to_col(tok_rows[i:i + 1]), (seqs, 128)).astype(jnp.int32) - first_id
    hid_copy.wait()

    @pl.loop(0, n_tiles)
    def _(tile):
        slot = lax.rem(tile, 2)
        w_copy(tile, slot).wait()

        @pl.when(tile + 1 < n_tiles)
        def _():
            w_copy(tile + 1, 1 - slot).start()

        @pl.loop(0, n_pos)
        def _(i):
            p_v[i, :, pl.ds(pl.multiple_of(tile * NT, NT), NT)] = INV_TEMP * jnp.dot(
                hid_v[i], w_v[slot], preferred_element_type=F32)

    def stats(i, rows):
        def tile_max(t, m):
            return jnp.maximum(m, jnp.max(p_v[i, :, pl.ds(pl.multiple_of(t * NT, NT), NT)], axis=1, keepdims=True))

        m = lax.fori_loop(0, n_tiles, tile_max, jnp.full((seqs, 1), -jnp.inf, F32))

        def tile_sum(t, s):
            return s + jnp.sum(jnp.exp(p_v[i, :, pl.ds(pl.multiple_of(t * NT, NT), NT)] - m), axis=1, keepdims=True)

        s = lax.fori_loop(0, n_tiles, tile_sum, jnp.zeros((seqs, 1), F32))
        return put_row(rows[0], i, to_row(m)), put_row(rows[1], i, to_row(s))

    max_rows, sum_rows = lax.fori_loop(0, n_pos, stats, (jnp.zeros((8, seqs), F32), jnp.zeros((8, seqs), F32)))
    stat_v[me, 0:8, :] = max_rows
    stat_v[me, 8:16, :] = sum_rows
    for k in range(8, 15):
        if k == 11:
            for j in range(15):
                small_copy(stat_v, s_send, s_recv, me, *peer(j)).start()
        q_copy(*peer(k)).start()
    for j in range(15):
        plane, core = peer(j)
        small_arrival(stat_v, s_send, s_recv, plane * nb + core).wait_recv()

    all_max = stat_v[0, 0:8, :]
    for k in range(1, n_peers):
        all_max = jnp.maximum(all_max, stat_v[k, 0:8, :])
    all_sum = jnp.zeros((8, seqs), F32)
    for k in range(n_peers):
        all_sum += stat_v[k, 8:16, :] * jnp.exp(stat_v[k, 0:8, :] - all_max)
    inv_sum = 1.0 / jnp.where(lax.broadcasted_iota(jnp.int32, (8, seqs), 0) < n_pos, all_sum, 1.0)

    def normalise(i, picked):
        m, r = to_col(get_row(all_max, i)), to_col(get_row(inv_sum, i))
        tok = tok_v[i, :, 0:1]

        def tile(t, got):
            cols = pl.ds(pl.multiple_of(t * NT, NT), NT)
            prob = jnp.exp(p_v[i, :, cols] - m) * r
            p_v[i, :, cols] = prob
            lane = lax.broadcasted_iota(jnp.int32, (seqs, NT), 1) + t * NT
            return got + jnp.sum(jnp.where(lane == tok, prob, 0.0), axis=1, keepdims=True)

        return put_row(picked, i, to_row(lax.fori_loop(0, n_tiles, tile, jnp.zeros((seqs, 1), F32))))

    p_pick = lax.fori_loop(0, n_draft, normalise, jnp.zeros((8, seqs), F32))
    m, r = to_col(get_row(all_max, n_draft)), to_col(get_row(inv_sum, n_draft))

    @pl.loop(0, n_tiles)
    def _(t):
        cols = pl.ds(pl.multiple_of(t * NT, NT), NT)
        bonus_ref[:, cols] = jnp.exp(p_v[n_draft, :, cols] - m) * r

    def absorb(other, carry):
        first = pl.multiple_of(other * local_seqs, 8)
        rows = pl.ds(first, local_seqs)
        lane = lax.broadcasted_iota(jnp.int32, (local_seqs, vocab), 1)
        place = (lax.broadcasted_iota(jnp.int32, (local_seqs, seqs), 1)
                 == lax.broadcasted_iota(jnp.int32, (local_seqs, seqs), 0) + first)

        def one(i, carry):
            z_rows, q_rows = carry
            q = ex_ref[i, rows, :]
            got = jnp.sum(jnp.where(lane == tok_v[i, rows, 0:1], q, 0.0), axis=1, keepdims=True)
            excess = jnp.maximum(p_v[i, rows, :] - q, 0.0)
            ex_ref[i, rows, :] = excess
            z = jnp.sum(excess, axis=1, keepdims=True)
            here = lax.broadcasted_iota(jnp.int32, (8, seqs), 0) == i
            z_rows += jnp.where(here, jnp.sum(jnp.where(place, z, 0.0), axis=0, keepdims=True), 0.0)
            q_rows += jnp.where(here, jnp.sum(jnp.where(place, got, 0.0), axis=0, keepdims=True), 0.0)
            return z_rows, q_rows

        return lax.fori_loop(0, n_draft, one, carry)

    own_copy.wait()
    carry = absorb(me, (jnp.zeros((8, seqs), F32), jnp.zeros((8, seqs), F32)))

    def arrived(k, carry):
        plane, core = peer(lax.rem(k + 12, 15))
        other = plane * nb + core
        q_arrival(other).wait_recv()
        return absorb(other, carry)

    z_rows, q_pick = lax.fori_loop(0, 15, arrived, carry)

    local_tok = tok_rows - first_id.astype(F32)
    owned = (local_tok >= 0.0) & (local_tok < float(vocab))
    ratio = jnp.minimum(1.0, p_pick[:n_draft] / jnp.where(owned, q_pick[:n_draft], 1.0))
    sums_ref[me, 0:8, :] = z_rows
    sums_ref[me, 8:16, :] = jnp.zeros((8, seqs), F32)
    sums_ref[me, 8:8 + n_draft, :] = jnp.where(owned, ratio, 0.0)
    for j in range(15):
        small_copy(sums_ref, z_send, z_recv, me, *peer(j)).start()
    for j in range(15):
        plane, core = peer(j)
        small_arrival(sums_ref, z_send, z_recv, plane * nb + core).wait_recv()
    for j in range(15):
        q_copy(*peer(j)).wait_send()
        small_copy(stat_v, s_send, s_recv, me, *peer(j)).wait_send()
        small_copy(sums_ref, z_send, z_recv, me, *peer(j)).wait_send()


SLOTS = 4


def output_kernel(n_peers, ex_ref, bonus_ref, sums_ref, res_ref, bonus_out, accept_ref, expected_ref, stage, stage_sem, bonus_sem):
    n_draft, seqs, vocab = ex_ref.shape
    half = seqs // 2
    bonus_copy = pltpu.make_async_copy(bonus_ref, bonus_out, bonus_sem)
    bonus_copy.start()
    total = sums_ref[0]
    for k in range(1, n_peers):
        total += sums_ref[k]
    inv = 1.0 / jnp.where(lax.broadcasted_iota(jnp.int32, (8, seqs), 0) < n_draft, total[0:8], 1.0)

    def out_copy(k, slot):
        i, h = k // 2, lax.rem(k, 2)
        return pltpu.make_async_copy(
            stage.at[slot], res_ref.at[i, pl.ds(pl.multiple_of(h * half, half), half), :], stage_sem.at[slot])

    @pl.loop(0, 2 * n_draft)
    def _(k):
        i, h, slot = k // 2, lax.rem(k, 2), lax.rem(k, SLOTS)
        row = get_row(inv, i)
        col = to_col(jnp.where(h == 0, row[:, :half], row[:, half:]))

        @pl.when(k >= SLOTS)
        def _():
            out_copy(k - SLOTS, slot).wait()

        @pl.loop(0, vocab // NT)
        def _(t):
            cols = pl.ds(pl.multiple_of(t * NT, NT), NT)
            stage[slot, :, cols] = ex_ref[i, pl.ds(pl.multiple_of(h * half, half), half), cols] * col

        out_copy(k, slot).start()

    accept = total[8:8 + n_draft]
    accept_ref[...] = accept
    prod = accept[0:1]
    expected = prod
    for i in range(1, n_draft):
        prod = prod * accept[i:i + 1]
        expected += prod
    expected_ref[...] = expected
    for k in range(2 * n_draft - SLOTS, 2 * n_draft):
        out_copy(k, k % SLOTS).wait()
    bonus_copy.wait()


def solution(mesh):
    na, nb = mesh.shape["tpa"], mesh.shape["tpb"]
    n_peers = na * nb
    any_spec = pl.BlockSpec(memory_space=pl.ANY)
    vmem_spec = pl.BlockSpec(memory_space=pltpu.VMEM)

    def local_step(hidden, w_head, q_draft, x_draft):
        seqs, n_pos, depth = hidden.shape
        vocab = w_head.shape[1]
        local_seqs, n_draft, _ = q_draft.shape
        dims = (n_pos, seqs, depth, vocab, local_seqs, na, nb)
        dma = pltpu.SemaphoreType.DMA
        ex, bonus, sums = pl.pallas_call(
            functools.partial(exchange_kernel, dims),
            out_shape=(pltpu.VMEM((n_draft, seqs, vocab), F32), pltpu.VMEM((seqs, vocab), F32),
                       pltpu.VMEM((n_peers, 16, seqs), F32)),
            in_specs=[any_spec, any_spec, any_spec, vmem_spec],
            out_specs=(vmem_spec, vmem_spec, vmem_spec),
            scratch_shapes=[
                pltpu.VMEM((n_pos, seqs, depth), jnp.bfloat16),
                pltpu.VMEM((2, depth, NT), jnp.bfloat16),
                pltpu.VMEM((n_pos, seqs, vocab), F32),
                pltpu.VMEM((n_draft, seqs, 128), jnp.int32),
                pltpu.VMEM((n_peers, 16, seqs), F32),
                dma, dma((2,)), dma,
                dma((n_peers,)), dma((n_peers,)), dma((n_peers,)), dma((n_peers,)), dma((n_peers,)), dma((n_peers,)),
            ],
            compiler_params=pltpu.CompilerParams(collective_id=0, has_side_effects=True, vmem_limit_bytes=38 * 2**20),
            name="exchange",
        )(hidden.transpose(1, 0, 2), w_head, q_draft.transpose(1, 0, 2), x_draft.T)
        res, bonus_out, accept, expected = pl.pallas_call(
            functools.partial(output_kernel, n_peers),
            out_shape=(jax.ShapeDtypeStruct((n_draft, seqs, vocab), F32), jax.ShapeDtypeStruct((seqs, vocab), F32),
                       jax.ShapeDtypeStruct((n_draft, seqs), F32), jax.ShapeDtypeStruct((1, seqs), F32)),
            in_specs=[vmem_spec, vmem_spec, vmem_spec],
            out_specs=(any_spec, any_spec, vmem_spec, vmem_spec),
            scratch_shapes=[pltpu.VMEM((SLOTS, seqs // 2, vocab), F32), dma((SLOTS,)), dma],
            compiler_params=pltpu.CompilerParams(vmem_limit_bytes=12 * 2**20),
            name="output",
        )(ex, bonus, sums)
        return accept.T, expected.reshape(seqs), res.transpose(1, 0, 2), bonus_out

    return jax.shard_map(
        local_step, mesh=mesh,
        in_specs=(P("dp", None, None), P(None, VOCAB_AXES), P(("dp",) + VOCAB_AXES, None, None), P("dp", None)),
        out_specs=(P("dp", None), P("dp"), P("dp", None, VOCAB_AXES), P("dp", VOCAB_AXES)),
        check_vma=False)
```

time: 1240 us -> 437 us (0.35); the launches traced: 1220 us -> 437 us
  local copies, waits for them, and re-layouts: 594 us -> 0 us
  blocking collectives: 478 us -> 0 us
  Pallas kernels: 0 us -> 436 us
  other arithmetic: 113 us -> 0 us
  matrix products: 30.3 us -> 0 us
    unnamed x16 -> x0, local copies, waits for them, and re-layouts: 443 us -> none
    pallas_call x0 -> x2, Pallas kernels: none -> 436 us  [the longest x1 428 us: local_step(): pl.pallas_call(functools.partial(exchange_kernel, dims), out_shape=(pltpu...]
    pmax x1 -> x0, blocking collectives: 338 us -> none  [local_step(): glob_max = lax.pmax(jnp.max(logits, axis=-1), VOCAB_AXES)]
    psum x2 -> x0, blocking collectives: 140 us -> none  [the longest x1 82.2 us: local_step(): exp_sum = lax.psum(jnp.sum(exp_vals, axis=-1), VOCAB_AXES)]
    all_to_all x2 -> x0, local copies, waits for them, and re-layouts: 103 us -> none  [local_step(): q_vocab = lax.all_to_all(q_draft, VOCAB_AXES, 2, 0, tiled=True)]
    all_to_all x1 -> x0, other arithmetic: 54.1 us -> none  [local_step(): q_vocab = lax.all_to_all(q_draft, VOCAB_AXES, 2, 0, tiled=True)]
    gather x5 -> x0, local copies, waits for them, and re-layouts: 45.7 us -> none  [the longest x2 23.1 us: local_step(): jnp.take_along_axis(q_vocab, safe_ids, axis=2)[..., 0]]
    dot_general x1 -> x0, matrix products: 30.3 us -> none  [local_step(): jnp.einsum('bgd,dv->bgv', hidden, w_head, preferred_element_type=jnp.floa...]
  transfers between devices with their start and end apart: 1 -> 0, of which waited for: 0 -> 0; matrix products, arithmetic and copies ran while one was open for 4% -> 0% of each run, Pallas kernels for 0% -> 0%
where the time goes in v1:
time: 437 us
  Pallas kernels  436 us (100%)
    pallas_call x1, Pallas kernels, local_step(): pl.pallas_call(functools.partial(exchange_kernel, dims), out_shape=(pltpu...  428 us

profile of v1, /device:TPU:0, one launch (start us, length us, event | category | flops | bytes accessed | tf_op | source)
XLA Modules:
  0.0 436.9 jit_solution(8760112300229322730)
XLA Ops:
  0.6 428.2 %exchange.1 = (f32[6,256,3072]{2,1,0:T(8,128)S(1)}, f32[256,3072]{1,0:T(8,128)S(1)}, f32[16,16,256]{2,1,0:T(8,128)S(1)}) custom-call(bf16[7,256,2048]{2,1,0:T(8,128)(2,1)} %bitcast.7, bf16[2048,3072]{1,0:T(8,128)(2,1)} %w_ref.1, f32[6,16,49152]{2,1,0:T(8,128)} %bitcast.6, s32[6,256]{1,0:T(8,128)} %bitcast.8), custom_call_target="tpu_custom_call" | custom-call | tf_op jit(solution)/shard_map/exchange/pallas_call | solution.py:297
  428.9 8.1 %output.1 = (f32[6,256,3072]{2,1,0:T(8,128)}, f32[256,3072]{1,0:T(8,128)}, f32[6,256]{1,0:T(8,128)}, f32[1,256]{1,0:T(1,128)}) custom-call(f32[6,256,3072]{2,1,0:T(8,128)S(1)} %get-tuple-element.11.ex_ref, f32[256,3072]{1,0:T(8,128)S(1)} %get-tuple-element.12.bonus_ref, f32[16,16,256]{2,1,0:T(8,128)S(1)} %get-tuple-element.13.sums_ref), custom_call_target="tpu_custom_call" | custom-call | tf_op jit(solution)/shard_map/output/pallas_call | solution.py:315

commit v2 on v0

v2 whole, which is shorter than its diff:
```python
import functools

import jax
import jax.numpy as jnp
from jax import lax
from jax.experimental import pallas as pl
from jax.experimental.pallas import tpu as pltpu
from jax.sharding import PartitionSpec as P

INV_TEMP = 1.25
VOCAB_AXES = ("tpa", "tpb")
MESH = pl.DeviceIdType.MESH
F32 = jnp.float32
SEND = ((3, 3, 0, 0), (1, 0, 3, 2), (2, 2, 1, 1))
RECV = ((3, 0, 3, 0), (2, 3, 0, 1), (1, 2, 1, 2))
CORE_OFFSETS = (0, 2, 1, 3)
NT = 512


def pick(index, values):
    out = jnp.int32(values[-1])
    for k in range(len(values) - 2, -1, -1):
        out = jnp.where(index == k, jnp.int32(values[k]), out)
    return out


def diag(n):
    return lax.broadcasted_iota(jnp.int32, (n, n), 0) == lax.broadcasted_iota(jnp.int32, (n, n), 1)


def to_col(row):
    return jnp.sum(jnp.where(diag(row.shape[1]), row, 0.0), axis=1, keepdims=True)


def get_row(rows, i):
    return jnp.sum(jnp.where(lax.broadcasted_iota(jnp.int32, rows.shape, 0) == i, rows, 0.0), axis=0, keepdims=True)


def lanes(n, first, rows):
    return (lax.broadcasted_iota(jnp.int32, (rows, n), 1)
            == lax.broadcasted_iota(jnp.int32, (rows, n), 0) + first)


def spread(col, n, first):
    return jnp.sum(jnp.where(lanes(n, first, col.shape[0]), col, 0.0), axis=0, keepdims=True)


def gather(row, first, rows):
    return jnp.sum(jnp.where(lanes(row.shape[1], first, rows), row, 0.0), axis=1, keepdims=True)


def exchange_kernel(dims, hid_ref, w_ref, q_ref, x_ref, ex_ref, bonus_ref, early_ref, late_ref,
                    hid_v, w_v, z_v, tok_v, stat_out, stat_in, norm_v, sum_out, sum_in, hid_sem, w_sem, own_sem,
                    q_send, q_recv, r_send, r_recv, so_send, so_recv, n_send, n_recv, zo_send, zo_recv,
                    e_send, e_recv, l_send, l_recv):
    n_pos, seqs, depth, vocab, n_loc, na, nb = dims
    n_draft = n_pos - 1
    n_early = n_draft - 1
    n_peers = na * nb
    n_tiles = vocab // NT
    others = range(n_peers - 1)
    dp, za, tb = lax.axis_index("dp"), lax.axis_index("tpa"), lax.axis_index("tpb")
    me = za * nb + tb

    def send_peer(k):
        inner = (za == 1) | (za == 2)
        if k < 3:
            end, mid = (pick(za, SEND[0]), CORE_OFFSETS[k]), (za, k + 1)
        else:
            mid = (pick(za, SEND[(k - 3) // nb]), CORE_OFFSETS[(k - 3) % nb])
            end = (pick(za, SEND[k // nb]), CORE_OFFSETS[k % nb]) if k < 12 else (za, k - 11)
        plane = jnp.where(inner, mid[0], end[0])
        return plane, lax.rem(tb + jnp.where(inner, mid[1], end[1]), nb)

    def recv_peer(k):
        step, off = (k - 3) // nb, lax.rem(jnp.int32(k) + 1, nb)
        plane = jnp.where(k < 3, za, jnp.where(step == 0, pick(za, RECV[0]),
                          jnp.where(step == 1, pick(za, RECV[1]), pick(za, RECV[2]))))
        off = jnp.where(k < 3, k + 1, nb - pick(off, CORE_OFFSETS))
        return plane, lax.rem(tb + off, nb)

    def rows_of(group):
        return pl.ds(pl.multiple_of(group * n_loc, 8), n_loc)

    def q_copy(part, plane, core, own_group, column):
        i0, ni = (0, n_early) if part == 0 else (n_early, 1)
        send, recv = (q_send, q_recv) if part == 0 else (r_send, r_recv)
        return pltpu.make_async_remote_copy(
            src_ref=q_ref.at[pl.ds(i0, ni), :, pl.ds(pl.multiple_of(column * vocab, 128), vocab)],
            dst_ref=ex_ref.at[pl.ds(i0, ni), rows_of(own_group), :],
            send_sem=send.at[plane * nb + core], recv_sem=recv.at[own_group],
            device_id=(dp, plane, core), device_id_type=MESH)

    def q_to(part, k):
        plane, core = send_peer(k)
        return q_copy(part, plane, core, me, plane * nb + core)

    def q_from(part, group):
        return q_copy(part, za, tb, group, 0)

    def small(src, dst, send, recv, src_slot, dst_slot, plane, core):
        return pltpu.make_async_remote_copy(
            src_ref=src.at[src_slot], dst_ref=dst.at[dst_slot],
            send_sem=send.at[plane * nb + core], recv_sem=recv.at[dst_slot],
            device_id=(dp, plane, core), device_id_type=MESH)

    def scatter_to(src, dst, send, recv, plane, core):
        return small(src, dst, send, recv, plane * nb + core, me, plane, core)

    def share_to(ref, send, recv, plane, core):
        return small(ref, ref, send, recv, me, me, plane, core)

    def await_all(ref, send, recv):
        for k in others:
            plane, core = send_peer(k)
            small(ref, ref, send, recv, plane * nb + core, plane * nb + core, za, tb).wait_recv()

    def w_copy(tile, slot):
        return pltpu.make_async_copy(w_ref.at[:, pl.ds(pl.multiple_of(tile * NT, NT), NT)], w_v.at[slot], w_sem.at[slot])

    hid_copy = pltpu.make_async_copy(hid_ref, hid_v, hid_sem)
    own_copy = pltpu.make_async_copy(
        q_ref.at[:, :, pl.ds(pl.multiple_of(me * vocab, 128), vocab)], ex_ref.at[:, rows_of(me), :], own_sem)

    barrier = pltpu.get_barrier_semaphore()
    for k in range(1, n_peers):
        pl.semaphore_signal(barrier, inc=1, device_id=(dp, lax.rem(za + k // nb, na), lax.rem(tb + k % nb, nb)),
                            device_id_type=MESH)
    pl.semaphore_wait(barrier, n_peers - 1)

    for k in range(4):
        q_to(0, k).start()
    hid_copy.start()
    w_copy(0, 0).start()
    own_copy.start()

    tok_rows = x_ref[...].astype(F32)
    for i in range(n_draft):
        tok_v[i] = jnp.broadcast_to(to_col(tok_rows[i:i + 1]), (seqs, 128)).astype(jnp.int32) - me * vocab
    hid_copy.wait()

    @pl.loop(0, n_tiles)
    def _(tile):
        slot = lax.rem(tile, 2)
        w_copy(tile, slot).wait()

        @pl.when(tile + 1 < n_tiles)
        def _():
            w_copy(tile + 1, 1 - slot).start()

        @pl.loop(0, n_pos)
        def _(i):
            z_v[i, :, pl.ds(pl.multiple_of(tile * NT, NT), NT)] = INV_TEMP * jnp.dot(
                hid_v[i], w_v[slot], preferred_element_type=F32)

    @pl.loop(0, n_peers)
    def _(group):
        def one(i, rows):
            z = z_v[i, rows_of(group), :]
            m = jnp.max(z, axis=1, keepdims=True)
            s = jnp.sum(jnp.exp(z - m), axis=1, keepdims=True)
            return rows[0] + spread(m, 128, i * n_loc), rows[1] + spread(s, 128, i * n_loc)

        zero = jnp.zeros((1, 128), F32)
        m_row, s_row = lax.fori_loop(0, n_pos, one, (zero, zero))
        stat_out[group] = jnp.concatenate([m_row, s_row], axis=0)

    stat_in[me] = stat_out[me]
    for k in others:
        scatter_to(stat_out, stat_in, so_send, so_recv, *send_peer(k)).start()
    for k in (4, 5):
        q_to(0, k).start()
    await_all(stat_in, so_send, so_recv)
    top = stat_in[0, 0:1, :]
    for k in range(1, n_peers):
        top = jnp.maximum(top, stat_in[k, 0:1, :])
    total = jnp.zeros((1, 128), F32)
    for k in range(n_peers):
        total += stat_in[k, 1:2, :] * jnp.exp(stat_in[k, 0:1, :] - top)
    used = lax.broadcasted_iota(jnp.int32, (1, 128), 1) < n_pos * n_loc
    norm_v[me] = jnp.concatenate([top, 1.0 / jnp.where(used, total, 1.0)], axis=0)
    for k in others:
        share_to(norm_v, n_send, n_recv, *send_peer(k)).start()
    for k in range(6, 15):
        q_to(0, k).start()
    for k in range(11):
        q_to(1, k).start()
    await_all(norm_v, n_send, n_recv)

    def probs(i, group):
        norm = norm_v[group]
        m, r = gather(norm[0:1], i * n_loc, n_loc), gather(norm[1:2], i * n_loc, n_loc)
        return jnp.exp(z_v[i, rows_of(group), :] - m) * r

    @pl.loop(0, n_peers)
    def _(group):
        bonus_ref[rows_of(group), :] = probs(n_draft, group)

    def cell(i, group):
        rows = rows_of(group)
        p, q, tok = probs(i, group), ex_ref[i, rows, :], tok_v[i, rows, 0:1]
        hit = lax.broadcasted_iota(jnp.int32, (n_loc, vocab), 1) == tok
        p_pick = jnp.sum(jnp.where(hit, p, 0.0), axis=1, keepdims=True)
        q_pick = jnp.sum(jnp.where(hit, q, 0.0), axis=1, keepdims=True)
        excess = jnp.maximum(p - q, 0.0)
        ex_ref[i, rows, :] = excess
        owned = (tok >= 0) & (tok < vocab)
        accept = jnp.where(owned, jnp.minimum(1.0, p_pick / jnp.where(owned, q_pick, 1.0)), 0.0)
        return jnp.sum(excess, axis=1, keepdims=True), accept

    def absorb_early(group):
        def one(i, rows):
            z, a = cell(i, group)
            return rows[0] + spread(z, 128, i * n_loc), rows[1] + spread(a, 128, i * n_loc)

        zero = jnp.zeros((1, 128), F32)
        z_row, a_row = lax.fori_loop(0, n_early, one, (zero, zero))
        sum_out[group] = jnp.concatenate([z_row, a_row], axis=0)

    own_copy.wait()
    absorb_early(me)
    sum_in[me] = sum_out[me]

    @pl.loop(0, n_peers - 1)
    def _(k):
        plane, core = recv_peer(k)
        group = plane * nb + core
        q_from(0, group).wait_recv()
        absorb_early(group)
        scatter_to(sum_out, sum_in, zo_send, zo_recv, plane, core).start()

    for k in range(11, 15):
        q_to(1, k).start()

    def absorb_late(group, rows):
        z, a = cell(n_early, group)
        return rows[0] + spread(z, seqs, group * n_loc), rows[1] + spread(a, seqs, group * n_loc)

    def arrived(k, rows):
        plane, core = recv_peer(k)
        q_from(1, plane * nb + core).wait_recv()
        return absorb_late(plane * nb + core, rows)

    zero = jnp.zeros((1, seqs), F32)
    rows = lax.fori_loop(0, 11, arrived, absorb_late(me, (zero, zero)))
    await_all(sum_in, zo_send, zo_recv)
    total = sum_in[0]
    for k in range(1, n_peers):
        total += sum_in[k]
    early_ref[me] = total
    rows = arrived(11, rows)
    for k in others:
        share_to(early_ref, e_send, e_recv, *send_peer(k)).start()
    rows = lax.fori_loop(12, 15, arrived, rows)

    late_ref[me] = jnp.concatenate(rows, axis=0)
    for k in others:
        q_to(0, k).wait_send()
        q_to(1, k).wait_send()
    for k in others:
        share_to(late_ref, l_send, l_recv, *send_peer(k)).start()
    await_all(early_ref, e_send, e_recv)
    await_all(late_ref, l_send, l_recv)
    for k in others:
        plane, core = send_peer(k)
        scatter_to(stat_out, stat_in, so_send, so_recv, plane, core).wait_send()
        share_to(norm_v, n_send, n_recv, plane, core).wait_send()
        scatter_to(sum_out, sum_in, zo_send, zo_recv, plane, core).wait_send()
        share_to(early_ref, e_send, e_recv, plane, core).wait_send()
        share_to(late_ref, l_send, l_recv, plane, core).wait_send()


SLOTS = 4


def output_kernel(n_peers, ex_ref, bonus_ref, early_ref, late_ref, res_ref, bonus_out, accept_ref, expected_ref,
                  stage, stage_sem, bonus_sem):
    n_draft, seqs, vocab = ex_ref.shape
    n_loc, half = seqs // n_peers, seqs // 2
    bonus_copy = pltpu.make_async_copy(bonus_ref, bonus_out, bonus_sem)
    bonus_copy.start()

    late = late_ref[0]
    for k in range(1, n_peers):
        late += late_ref[k]
    lane = lax.broadcasted_iota(jnp.int32, (n_peers, 128), 1)
    mine = (lax.broadcasted_iota(jnp.int32, (n_peers, seqs), 1) // n_loc
            == lax.broadcasted_iota(jnp.int32, (n_peers, seqs), 0))

    def by_position(which):
        table = jnp.concatenate([early_ref[g, which:which + 1, :] for g in range(n_peers)], axis=0)
        out = jnp.broadcast_to(late[which:which + 1], (8, seqs))
        for i in range(n_draft - 1):
            x = pltpu.roll(table, (128 - n_loc * i) % 128, 1)
            x = jnp.where(lane < n_loc, x, 0.0)
            shift = n_loc
            while shift < 128:
                x = x + pltpu.roll(x, shift, 1)
                shift *= 2
            x = jnp.concatenate([x] * (seqs // 128), axis=1)
            row = jnp.sum(jnp.where(mine, x, 0.0), axis=0, keepdims=True)
            out = jnp.where(lax.broadcasted_iota(jnp.int32, (8, seqs), 0) == i, row, out)
        return out

    inv = 1.0 / by_position(0)

    def out_copy(k, slot):
        i, h = k // 2, lax.rem(k, 2)
        return pltpu.make_async_copy(
            stage.at[slot], res_ref.at[i, pl.ds(pl.multiple_of(h * half, half), half), :], stage_sem.at[slot])

    @pl.loop(0, 2 * n_draft)
    def _(k):
        i, h, slot = k // 2, lax.rem(k, 2), lax.rem(k, SLOTS)
        row = get_row(inv, i)
        col = to_col(jnp.where(h == 0, row[:, :half], row[:, half:]))

        @pl.when(k >= SLOTS)
        def _():
            out_copy(k - SLOTS, slot).wait()

        @pl.loop(0, vocab // NT)
        def _(t):
            cols = pl.ds(pl.multiple_of(t * NT, NT), NT)
            stage[slot, :, cols] = ex_ref[i, pl.ds(pl.multiple_of(h * half, half), half), cols] * col

        out_copy(k, slot).start()

    accept = by_position(1)[:n_draft]
    accept_ref[...] = accept
    prod = accept[0:1]
    expected = prod
    for i in range(1, n_draft):
        prod = prod * accept[i:i + 1]
        expected += prod
    expected_ref[...] = expected
    for k in range(2 * n_draft - SLOTS, 2 * n_draft):
        out_copy(k, k % SLOTS).wait()
    bonus_copy.wait()


def solution(mesh):
    na, nb = mesh.shape["tpa"], mesh.shape["tpb"]
    n_peers = na * nb
    any_spec = pl.BlockSpec(memory_space=pl.ANY)
    vmem_spec = pl.BlockSpec(memory_space=pltpu.VMEM)

    def local_step(hidden, w_head, q_draft, x_draft):
        seqs, n_pos, depth = hidden.shape
        vocab = w_head.shape[1]
        n_loc, n_draft, _ = q_draft.shape
        dims = (n_pos, seqs, depth, vocab, n_loc, na, nb)
        dma = pltpu.SemaphoreType.DMA
        small = pltpu.VMEM((n_peers, 2, 128), F32)
        ex, bonus, early, late = pl.pallas_call(
            functools.partial(exchange_kernel, dims),
            out_shape=(pltpu.VMEM((n_draft, seqs, vocab), F32), pltpu.VMEM((seqs, vocab), F32),
                       small, pltpu.VMEM((n_peers, 2, seqs), F32)),
            in_specs=[any_spec, any_spec, any_spec, vmem_spec],
            out_specs=(vmem_spec,) * 4,
            scratch_shapes=[
                pltpu.VMEM((n_pos, seqs, depth), jnp.bfloat16),
                pltpu.VMEM((2, depth, NT), jnp.bfloat16),
                pltpu.VMEM((n_pos, seqs, vocab), F32),
                pltpu.VMEM((n_draft, seqs, 128), jnp.int32),
                small, small, small, small, small,
                dma, dma((2,)), dma,
            ] + [dma((n_peers,))] * 14,
            compiler_params=pltpu.CompilerParams(collective_id=0, has_side_effects=True, vmem_limit_bytes=38 * 2**20),
            name="exchange",
        )(hidden.transpose(1, 0, 2), w_head, q_draft.transpose(1, 0, 2), x_draft.T)
        res, bonus_out, accept, expected = pl.pallas_call(
            functools.partial(output_kernel, n_peers),
            out_shape=(jax.ShapeDtypeStruct((n_draft, seqs, vocab), F32), jax.ShapeDtypeStruct((seqs, vocab), F32),
                       jax.ShapeDtypeStruct((n_draft, seqs), F32), jax.ShapeDtypeStruct((1, seqs), F32)),
            in_specs=[vmem_spec] * 4,
            out_specs=(any_spec, any_spec, vmem_spec, vmem_spec),
            scratch_shapes=[pltpu.VMEM((SLOTS, seqs // 2, vocab), F32), dma((SLOTS,)), dma],
            compiler_params=pltpu.CompilerParams(vmem_limit_bytes=12 * 2**20),
            name="output",
        )(ex, bonus, early, late)
        return accept.T, expected.reshape(seqs), res.transpose(1, 0, 2), bonus_out

    return jax.shard_map(
        local_step, mesh=mesh,
        in_specs=(P("dp", None, None), P(None, VOCAB_AXES), P(("dp",) + VOCAB_AXES, None, None), P("dp", None)),
        out_specs=(P("dp", None), P("dp"), P("dp", None, VOCAB_AXES), P("dp", VOCAB_AXES)),
        check_vma=False)
```

time: 1240 us -> 430 us (0.35); the launches traced: 1220 us -> 430 us
  local copies, waits for them, and re-layouts: 594 us -> 0 us
  blocking collectives: 478 us -> 0 us
  Pallas kernels: 0 us -> 429 us
  other arithmetic: 113 us -> 0 us
  matrix products: 30.3 us -> 0 us
    unnamed x16 -> x0, local copies, waits for them, and re-layouts: 443 us -> none
    pallas_call x0 -> x2, Pallas kernels: none -> 429 us  [the longest x1 421 us: local_step(): pl.pallas_call(functools.partial(exchange_kernel, dims), out_shape=(pltpu...]
    pmax x1 -> x0, blocking collectives: 338 us -> none  [local_step(): glob_max = lax.pmax(jnp.max(logits, axis=-1), VOCAB_AXES)]
    psum x2 -> x0, blocking collectives: 140 us -> none  [the longest x1 82.2 us: local_step(): exp_sum = lax.psum(jnp.sum(exp_vals, axis=-1), VOCAB_AXES)]
    all_to_all x2 -> x0, local copies, waits for them, and re-layouts: 103 us -> none  [local_step(): q_vocab = lax.all_to_all(q_draft, VOCAB_AXES, 2, 0, tiled=True)]
    all_to_all x1 -> x0, other arithmetic: 54.1 us -> none  [local_step(): q_vocab = lax.all_to_all(q_draft, VOCAB_AXES, 2, 0, tiled=True)]
    gather x5 -> x0, local copies, waits for them, and re-layouts: 45.7 us -> none  [the longest x2 23.1 us: local_step(): jnp.take_along_axis(q_vocab, safe_ids, axis=2)[..., 0]]
    dot_general x1 -> x0, matrix products: 30.3 us -> none  [local_step(): jnp.einsum('bgd,dv->bgv', hidden, w_head, preferred_element_type=jnp.floa...]
  transfers between devices with their start and end apart: 1 -> 0, of which waited for: 0 -> 0; matrix products, arithmetic and copies ran while one was open for 4% -> 0% of each run, Pallas kernels for 0% -> 0%
where the time goes in v2:
time: 430 us
  Pallas kernels  429 us (100%)
    pallas_call x1, Pallas kernels, local_step(): pl.pallas_call(functools.partial(exchange_kernel, dims), out_shape=(pltpu...  421 us

profile of v2, /device:TPU:0, one launch (start us, length us, event | category | flops | bytes accessed | tf_op | source)
XLA Modules:
  0.0 429.9 jit_solution(14293524237298365136)
XLA Ops:
  0.6 421.1 %exchange.1 = (f32[6,256,3072]{2,1,0:T(8,128)S(1)}, f32[256,3072]{1,0:T(8,128)S(1)}, f32[16,2,128]{2,1,0:T(2,128)S(1)}, f32[16,2,256]{2,1,0:T(2,128)S(1)}) custom-call(bf16[7,256,2048]{2,1,0:T(8,128)(2,1)} %bitcast.7, bf16[2048,3072]{1,0:T(8,128)(2,1)} %w_ref.1, f32[6,16,49152]{2,1,0:T(8,128)} %bitcast.6, s32[6,256]{1,0:T(8,128)} %bitcast.8), custom_call_target="tpu_custom_call" | custom-call | tf_op jit(solution)/shard_map/exchange/pallas_call | solution.py:355
  421.8 8.1 %output.1 = (f32[6,256,3072]{2,1,0:T(8,128)}, f32[256,3072]{1,0:T(8,128)}, f32[6,256]{1,0:T(8,128)}, f32[1,256]{1,0:T(1,128)}) custom-call(f32[6,256,3072]{2,1,0:T(8,128)S(1)} %get-tuple-element.12.ex_ref, f32[256,3072]{1,0:T(8,128)S(1)} %get-tuple-element.13.bonus_ref, f32[16,2,128]{2,1,0:T(2,128)S(1)} %get-tuple-element.14.early_ref, ...), custom_call_target="tpu_custom_call" | custom-call | tf_op jit(solution)/shard_map/output/pallas_call | solution.py:372

commit v3 on v2

--- a/solution.py
+++ b/solution.py
@@ -50,9 +50,9 @@
 
 
 def exchange_kernel(dims, hid_ref, w_ref, q_ref, x_ref, ex_ref, bonus_ref, early_ref, late_ref,
-                    hid_v, w_v, z_v, tok_v, stat_out, stat_in, norm_v, sum_out, sum_in, hid_sem, w_sem, own_sem,
-                    q_send, q_recv, r_send, r_recv, so_send, so_recv, n_send, n_recv, zo_send, zo_recv,
-                    e_send, e_recv, l_send, l_recv):
+                    hid_v, w_v, z_v, tok_v, stat_out, stat_1, stat_2, norm_v, sum_out, sum_1, sum_2, hid_sem, w_sem, own_sem,
+                    q_send, q_recv, r_recv, l_send, l_recv,
+                    a1_send, a1_recv, a2_send, a2_recv, a3_send, a3_recv, b1_send, b1_recv, b2_send, b2_recv, b3_send, b3_recv):
     n_pos, seqs, depth, vocab, n_loc, na, nb = dims
     n_draft = n_pos - 1
     n_early = n_draft - 1
@@ -84,36 +84,64 @@
 
     def q_copy(part, plane, core, own_group, column):
         i0, ni = (0, n_early) if part == 0 else (n_early, 1)
-        send, recv = (q_send, q_recv) if part == 0 else (r_send, r_recv)
+        recv = q_recv.at[own_group // nb] if part == 0 else r_recv.at[own_group]
         return pltpu.make_async_remote_copy(
             src_ref=q_ref.at[pl.ds(i0, ni), :, pl.ds(pl.multiple_of(column * vocab, 128), vocab)],
             dst_ref=ex_ref.at[pl.ds(i0, ni), rows_of(own_group), :],
-            send_sem=send.at[plane * nb + core], recv_sem=recv.at[own_group],
+            send_sem=q_send, recv_sem=recv,
             device_id=(dp, plane, core), device_id_type=MESH)
 
     def q_to(part, k):
         plane, core = send_peer(k)
         return q_copy(part, plane, core, me, plane * nb + core)
 
-    def q_from(part, group):
-        return q_copy(part, za, tb, group, 0)
+    def q_from_plane(plane, count):
+        rows = ex_ref.at[pl.ds(0, n_early), pl.ds(0, count * n_loc), :]
+        pltpu.make_async_copy(rows, rows, q_recv.at[plane]).wait()
+
+    def q_from(group):
+        return q_copy(1, za, tb, group, 0)
 
     def small(src, dst, send, recv, src_slot, dst_slot, plane, core):
         return pltpu.make_async_remote_copy(
-            src_ref=src.at[src_slot], dst_ref=dst.at[dst_slot],
-            send_sem=send.at[plane * nb + core], recv_sem=recv.at[dst_slot],
+            src_ref=src.at[src_slot], dst_ref=dst.at[dst_slot], send_sem=send, recv_sem=recv,
             device_id=(dp, plane, core), device_id_type=MESH)
 
-    def scatter_to(src, dst, send, recv, plane, core):
-        return small(src, dst, send, recv, plane * nb + core, me, plane, core)
-
-    def share_to(ref, send, recv, plane, core):
-        return small(ref, ref, send, recv, me, me, plane, core)
-
-    def await_all(ref, send, recv):
-        for k in others:
-            plane, core = send_peer(k)
-            small(ref, ref, send, recv, plane * nb + core, plane * nb + core, za, tb).wait_recv()
+    def await_slots(ref, sem, count):
+        part = ref.at[pl.ds(0, count)]
+        pltpu.make_async_copy(part, part, sem).wait()
+
+    def in_plane(src, dst, send, recv, scatter):
+        cores = [lax.rem(tb + k, nb) for k in range(1, nb)]
+        return [small(src, dst, send, recv, core if scatter else tb, tb, za, core) for core in cores]
+
+    def across(ref, send, recv):
+        planes = [lax.rem(za + k, na) for k in range(1, na)]
+        return [small(ref, ref, send, recv, za, za, plane, tb) for plane in planes]
+
+    def late_to(k):
+        plane, core = send_peer(k)
+        return small(late_ref, late_ref, l_send, l_recv, me, me, plane, core)
+
+    def start(copies):
+        for copy in copies:
+            copy.start()
+
+    def combine(ref):
+        top = ref[0, 0:4]
+        for k in range(1, 4):
+            top = jnp.maximum(top, ref[k, 0:4])
+        total = ref[0, 4:8] * jnp.exp(ref[0, 0:4] - top)
+        for k in range(1, 4):
+            total += ref[k, 4:8] * jnp.exp(ref[k, 0:4] - top)
+        return top, total
+
+    def add(ref):
+        return (ref[0] + ref[1]) + (ref[2] + ref[3])
+
+    def put(tile, plane, first, second):
+        row = lax.broadcasted_iota(jnp.int32, tile.shape, 0)
+        return jnp.where(row == plane, first, jnp.where(row == na + plane, second, tile))
 
     def w_copy(tile, slot):
         return pltpu.make_async_copy(w_ref.at[:, pl.ds(pl.multiple_of(tile * NT, NT), NT)], w_v.at[slot], w_sem.at[slot])
@@ -153,43 +181,42 @@
             z_v[i, :, pl.ds(pl.multiple_of(tile * NT, NT), NT)] = INV_TEMP * jnp.dot(
                 hid_v[i], w_v[slot], preferred_element_type=F32)
 
-    @pl.loop(0, n_peers)
-    def _(group):
-        def one(i, rows):
-            z = z_v[i, rows_of(group), :]
-            m = jnp.max(z, axis=1, keepdims=True)
-            s = jnp.sum(jnp.exp(z - m), axis=1, keepdims=True)
-            return rows[0] + spread(m, 128, i * n_loc), rows[1] + spread(s, 128, i * n_loc)
-
-        zero = jnp.zeros((1, 128), F32)
-        m_row, s_row = lax.fori_loop(0, n_pos, one, (zero, zero))
-        stat_out[group] = jnp.concatenate([m_row, s_row], axis=0)
-
-    stat_in[me] = stat_out[me]
-    for k in others:
-        scatter_to(stat_out, stat_in, so_send, so_recv, *send_peer(k)).start()
+    @pl.loop(0, nb)
+    def _(core):
+        def plane_rows(plane, tile):
+            def one(i, rows):
+                z = z_v[i, rows_of(plane * nb + core), :]
+                m = jnp.max(z, axis=1, keepdims=True)
+                s = jnp.sum(jnp.exp(z - m), axis=1, keepdims=True)
+                return rows[0] + spread(m, 128, i * n_loc), rows[1] + spread(s, 128, i * n_loc)
+
+            zero = jnp.zeros((1, 128), F32)
+            return put(tile, plane, *lax.fori_loop(0, n_pos, one, (zero, zero)))
+
+        stat_out[core] = lax.fori_loop(0, na, plane_rows, jnp.zeros((8, 128), F32))
+
+    stat_1[tb] = stat_out[tb]
+    start(in_plane(stat_out, stat_1, a1_send, a1_recv, True))
+    await_slots(stat_1, a1_recv, 3)
+    stat_2[za] = jnp.concatenate(combine(stat_1), axis=0)
+    start(across(stat_2, a2_send, a2_recv))
     for k in (4, 5):
         q_to(0, k).start()
-    await_all(stat_in, so_send, so_recv)
-    top = stat_in[0, 0:1, :]
-    for k in range(1, n_peers):
-        top = jnp.maximum(top, stat_in[k, 0:1, :])
-    total = jnp.zeros((1, 128), F32)
-    for k in range(n_peers):
-        total += stat_in[k, 1:2, :] * jnp.exp(stat_in[k, 0:1, :] - top)
-    used = lax.broadcasted_iota(jnp.int32, (1, 128), 1) < n_pos * n_loc
-    norm_v[me] = jnp.concatenate([top, 1.0 / jnp.where(used, total, 1.0)], axis=0)
-    for k in others:
-        share_to(norm_v, n_send, n_recv, *send_peer(k)).start()
+    await_slots(stat_2, a2_recv, 3)
+    top, total = combine(stat_2)
+    used = lax.broadcasted_iota(jnp.int32, (4, 128), 1) < n_pos * n_loc
+    norm_v[tb] = jnp.concatenate([top, 1.0 / jnp.where(used, total, 1.0)], axis=0)
+    start(in_plane(norm_v, norm_v, a3_send, a3_recv, False))
     for k in range(6, 15):
         q_to(0, k).start()
     for k in range(11):
         q_to(1, k).start()
-    await_all(norm_v, n_send, n_recv)
+    await_slots(norm_v, a3_recv, 3)
 
     def probs(i, group):
-        norm = norm_v[group]
-        m, r = gather(norm[0:1], i * n_loc, n_loc), gather(norm[1:2], i * n_loc, n_loc)
+        norm, plane = norm_v[lax.rem(group, nb)], group // nb
+        m = gather(get_row(norm, plane), i * n_loc, n_loc)
+        r = gather(get_row(norm, na + plane), i * n_loc, n_loc)
         return jnp.exp(z_v[i, rows_of(group), :] - m) * r
 
     @pl.loop(0, n_peers)
@@ -215,21 +242,34 @@
 
         zero = jnp.zeros((1, 128), F32)
         z_row, a_row = lax.fori_loop(0, n_early, one, (zero, zero))
-        sum_out[group] = jnp.concatenate([z_row, a_row], axis=0)
-
+        core = lax.rem(group, nb)
+        sum_out[core] = put(sum_out[core], group // nb, z_row, a_row)
+
+    sum_out[...] = jnp.zeros_like(sum_out)
     own_copy.wait()
     absorb_early(me)
-    sum_in[me] = sum_out[me]
-
-    @pl.loop(0, n_peers - 1)
-    def _(k):
-        plane, core = recv_peer(k)
-        group = plane * nb + core
-        q_from(0, group).wait_recv()
-        absorb_early(group)
-        scatter_to(sum_out, sum_in, zo_send, zo_recv, plane, core).start()
-
-    for k in range(11, 15):
+
+    q_from_plane(za, nb - 1)
+    for k in range(1, nb):
+        absorb_early(za * nb + lax.rem(tb + k, nb))
+
+    @pl.loop(0, na - 1)
+    def _(step):
+        plane = jnp.where(step == 0, pick(za, RECV[0]), jnp.where(step == 1, pick(za, RECV[1]), pick(za, RECV[2])))
+        q_from_plane(plane, nb)
+
+        @pl.loop(0, nb)
+        def _(core):
+            absorb_early(plane * nb + core)
+
+    sum_1[tb] = sum_out[tb]
+    start(in_plane(sum_out, sum_1, b1_send, b1_recv, True))
+    for k in (11, 12):
+        q_to(1, k).start()
+    await_slots(sum_1, b1_recv, 3)
+    sum_2[za] = add(sum_1)
+    start(across(sum_2, b2_send, b2_recv))
+    for k in (13, 14):
         q_to(1, k).start()
 
     def absorb_late(group, rows):
@@ -238,44 +278,36 @@
 
     def arrived(k, rows):
         plane, core = recv_peer(k)
-        q_from(1, plane * nb + core).wait_recv()
+        q_from(plane * nb + core).wait_recv()
         return absorb_late(plane * nb + core, rows)
 
     zero = jnp.zeros((1, seqs), F32)
     rows = lax.fori_loop(0, 11, arrived, absorb_late(me, (zero, zero)))
-    await_all(sum_in, zo_send, zo_recv)
-    total = sum_in[0]
-    for k in range(1, n_peers):
-        total += sum_in[k]
-    early_ref[me] = total
-    rows = arrived(11, rows)
+    await_slots(sum_2, b2_recv, 3)
+    early_ref[tb] = add(sum_2)
+    start(in_plane(early_ref, early_ref, b3_send, b3_recv, False))
+    rows = lax.fori_loop(11, 15, arrived, rows)
+
+    late_ref[me] = jnp.concatenate(rows, axis=0)
+    sent = q_ref.at[:, :, pl.ds(0, (n_peers - 1) * vocab)]
+    pltpu.make_async_copy(sent, sent, q_send).wait()
     for k in others:
-        share_to(early_ref, e_send, e_recv, *send_peer(k)).start()
-    rows = lax.fori_loop(12, 15, arrived, rows)
-
-    late_ref[me] = jnp.concatenate(rows, axis=0)
-    for k in others:
-        q_to(0, k).wait_send()
-        q_to(1, k).wait_send()
-    for k in others:
-        share_to(late_ref, l_send, l_recv, *send_peer(k)).start()
-    await_all(early_ref, e_send, e_recv)
-    await_all(late_ref, l_send, l_recv)
-    for k in others:
-        plane, core = send_peer(k)
-        scatter_to(stat_out, stat_in, so_send, so_recv, plane, core).wait_send()
-        share_to(norm_v, n_send, n_recv, plane, core).wait_send()
-        scatter_to(sum_out, sum_in, zo_send, zo_recv, plane, core).wait_send()
-        share_to(early_ref, e_send, e_recv, plane, core).wait_send()
-        share_to(late_ref, l_send, l_recv, plane, core).wait_send()
+        late_to(k).start()
+    await_slots(early_ref, b3_recv, 3)
+    await_slots(late_ref, l_recv, n_peers - 1)
+    await_slots(late_ref, l_send, n_peers - 1)
+    for ref, sem in ((stat_1, a1_send), (stat_2, a2_send), (norm_v, a3_send), (sum_1, b1_send), (sum_2, b2_send),
+                     (early_ref, b3_send)):
+        await_slots(ref, sem, 3)
 
 
 SLOTS = 4
 
 
-def output_kernel(n_peers, ex_ref, bonus_ref, early_ref, late_ref, res_ref, bonus_out, accept_ref, expected_ref,
+def output_kernel(na, nb, ex_ref, bonus_ref, early_ref, late_ref, res_ref, bonus_out, accept_ref, expected_ref,
                   stage, stage_sem, bonus_sem):
     n_draft, seqs, vocab = ex_ref.shape
+    n_peers = na * nb
     n_loc, half = seqs // n_peers, seqs // 2
     bonus_copy = pltpu.make_async_copy(bonus_ref, bonus_out, bonus_sem)
     bonus_copy.start()
@@ -288,7 +320,8 @@
             == lax.broadcasted_iota(jnp.int32, (n_peers, seqs), 0))
 
     def by_position(which):
-        table = jnp.concatenate([early_ref[g, which:which + 1, :] for g in range(n_peers)], axis=0)
+        table = jnp.concatenate(
+            [early_ref[g % nb, na * which + g // nb:na * which + g // nb + 1, :] for g in range(n_peers)], axis=0)
         out = jnp.broadcast_to(late[which:which + 1], (8, seqs))
         for i in range(n_draft - 1):
             x = pltpu.roll(table, (128 - n_loc * i) % 128, 1)
@@ -351,7 +384,7 @@
         n_loc, n_draft, _ = q_draft.shape
         dims = (n_pos, seqs, depth, vocab, n_loc, na, nb)
         dma = pltpu.SemaphoreType.DMA
-        small = pltpu.VMEM((n_peers, 2, 128), F32)
+        small = pltpu.VMEM((4, 8, 128), F32)
         ex, bonus, early, late = pl.pallas_call(
             functools.partial(exchange_kernel, dims),
             out_shape=(pltpu.VMEM((n_draft, seqs, vocab), F32), pltpu.VMEM((seqs, vocab), F32),
@@ -363,14 +396,14 @@
                 pltpu.VMEM((2, depth, NT), jnp.bfloat16),
                 pltpu.VMEM((n_pos, seqs, vocab), F32),
                 pltpu.VMEM((n_draft, seqs, 128), jnp.int32),
-                small, small, small, small, small,
-                dma, dma((2,)), dma,
-            ] + [dma((n_peers,))] * 14,
+                small, small, small, small, small, small, small,
+                dma, dma((2,)), dma, dma, dma((na,)), dma((n_peers,)),
+            ] + [dma] * 14,
             compiler_params=pltpu.CompilerParams(collective_id=0, has_side_effects=True, vmem_limit_bytes=38 * 2**20),
             name="exchange",
         )(hidden.transpose(1, 0, 2), w_head, q_draft.transpose(1, 0, 2), x_draft.T)
         res, bonus_out, accept, expected = pl.pallas_call(
-            functools.partial(output_kernel, n_peers),
+            functools.partial(output_kernel, na, nb),
             out_shape=(jax.ShapeDtypeStruct((n_draft, seqs, vocab), F32), jax.ShapeDtypeStruct((seqs, vocab), F32),
                        jax.ShapeDtypeStruct((n_draft, seqs), F32), jax.ShapeDtypeStruct((1, seqs), F32)),
             in_specs=[vmem_spec] * 4,

time: 430 us -> 427 us (level)
  no operation moved by 1% of the time
where the time goes in v3:
time: 427 us
  Pallas kernels  426 us (100%)
    pallas_call x1, Pallas kernels, local_step(): pl.pallas_call(functools.partial(exchange_kernel, dims), out_shape=(pltpu...  418 us

profile of v3, /device:TPU:0, one launch (start us, length us, event | category | flops | bytes accessed | tf_op | source)
XLA Modules:
  0.0 426.8 jit_solution(3163529960231219892)
XLA Ops:
  0.6 418.1 %exchange.1 = (f32[6,256,3072]{2,1,0:T(8,128)S(1)}, f32[256,3072]{1,0:T(8,128)S(1)}, f32[4,8,128]{2,1,0:T(8,128)S(1)}, f32[16,2,256]{2,1,0:T(2,128)S(1)}) custom-call(bf16[7,256,2048]{2,1,0:T(8,128)(2,1)} %bitcast.7, bf16[2048,3072]{1,0:T(8,128)(2,1)} %w_ref.1, f32[6,16,49152]{2,1,0:T(8,128)} %bitcast.6, s32[6,256]{1,0:T(8,128)} %bitcast.8), custom_call_target="tpu_custom_call" | custom-call | tf_op jit(solution)/shard_map/exchange/pallas_call | solution.py:388
  418.7 8.1 %output.1 = (f32[6,256,3072]{2,1,0:T(8,128)}, f32[256,3072]{1,0:T(8,128)}, f32[6,256]{1,0:T(8,128)}, f32[1,256]{1,0:T(1,128)}) custom-call(f32[6,256,3072]{2,1,0:T(8,128)S(1)} %get-tuple-element.12.ex_ref, f32[256,3072]{1,0:T(8,128)S(1)} %get-tuple-element.13.bonus_ref, f32[4,8,128]{2,1,0:T(8,128)S(1)} %get-tuple-element.14.early_ref, ...), custom_call_target="tpu_custom_call" | custom-call | tf_op jit(solution)/shard_map/output/pallas_call | solution.py:405

commit v4 on v3

--- a/solution.py
+++ b/solution.py
@@ -50,7 +50,7 @@
 
 
 def exchange_kernel(dims, hid_ref, w_ref, q_ref, x_ref, ex_ref, bonus_ref, early_ref, late_ref,
-                    hid_v, w_v, z_v, tok_v, stat_out, stat_1, stat_2, norm_v, sum_out, sum_1, sum_2, hid_sem, w_sem, own_sem,
+                    hid_v, w_v, z_v, x_v, tok_v, stat_out, stat_1, stat_2, norm_v, sum_out, sum_1, sum_2, hid_sem, w_sem, own_sem, x_sem,
                     q_send, q_recv, r_recv, l_send, l_recv,
                     a1_send, a1_recv, a2_send, a2_recv, a3_send, a3_recv, b1_send, b1_recv, b2_send, b2_recv, b3_send, b3_recv):
     n_pos, seqs, depth, vocab, n_loc, na, nb = dims
@@ -147,6 +147,7 @@
         return pltpu.make_async_copy(w_ref.at[:, pl.ds(pl.multiple_of(tile * NT, NT), NT)], w_v.at[slot], w_sem.at[slot])
 
     hid_copy = pltpu.make_async_copy(hid_ref, hid_v, hid_sem)
+    x_copy = pltpu.make_async_copy(x_ref, x_v, x_sem)
     own_copy = pltpu.make_async_copy(
         q_ref.at[:, :, pl.ds(pl.multiple_of(me * vocab, 128), vocab)], ex_ref.at[:, rows_of(me), :], own_sem)
 
@@ -158,11 +159,13 @@
 
     for k in range(4):
         q_to(0, k).start()
+    x_copy.start()
     hid_copy.start()
     w_copy(0, 0).start()
     own_copy.start()
 
-    tok_rows = x_ref[...].astype(F32)
+    x_copy.wait()
+    tok_rows = x_v[...].astype(F32)
     for i in range(n_draft):
         tok_v[i] = jnp.broadcast_to(to_col(tok_rows[i:i + 1]), (seqs, 128)).astype(jnp.int32) - me * vocab
     hid_copy.wait()
@@ -305,7 +308,7 @@
 
 
 def output_kernel(na, nb, ex_ref, bonus_ref, early_ref, late_ref, res_ref, bonus_out, accept_ref, expected_ref,
-                  stage, stage_sem, bonus_sem):
+                  stage, accept_v, expected_v, stage_sem, bonus_sem, small_sem):
     n_draft, seqs, vocab = ex_ref.shape
     n_peers = na * nb
     n_loc, half = seqs // n_peers, seqs // 2
@@ -360,16 +363,22 @@
         out_copy(k, slot).start()
 
     accept = by_position(1)[:n_draft]
-    accept_ref[...] = accept
+    accept_v[...] = accept
     prod = accept[0:1]
     expected = prod
     for i in range(1, n_draft):
         prod = prod * accept[i:i + 1]
         expected += prod
-    expected_ref[...] = expected
+    expected_v[...] = expected
+    small_copies = (pltpu.make_async_copy(accept_v, accept_ref, small_sem.at[0]),
+                    pltpu.make_async_copy(expected_v, expected_ref, small_sem.at[1]))
+    for copy in small_copies:
+        copy.start()
     for k in range(2 * n_draft - SLOTS, 2 * n_draft):
         out_copy(k, k % SLOTS).wait()
     bonus_copy.wait()
+    for copy in small_copies:
+        copy.wait()
 
 
 def solution(mesh):
@@ -389,15 +398,16 @@
             functools.partial(exchange_kernel, dims),
             out_shape=(pltpu.VMEM((n_draft, seqs, vocab), F32), pltpu.VMEM((seqs, vocab), F32),
                        small, pltpu.VMEM((n_peers, 2, seqs), F32)),
-            in_specs=[any_spec, any_spec, any_spec, vmem_spec],
+            in_specs=[any_spec] * 4,
             out_specs=(vmem_spec,) * 4,
             scratch_shapes=[
                 pltpu.VMEM((n_pos, seqs, depth), jnp.bfloat16),
                 pltpu.VMEM((2, depth, NT), jnp.bfloat16),
                 pltpu.VMEM((n_pos, seqs, vocab), F32),
+                pltpu.VMEM((n_draft, seqs), jnp.int32),
                 pltpu.VMEM((n_draft, seqs, 128), jnp.int32),
                 small, small, small, small, small, small, small,
-                dma, dma((2,)), dma, dma, dma((na,)), dma((n_peers,)),
+                dma, dma((2,)), dma, dma, dma, dma((na,)), dma((n_peers,)),
             ] + [dma] * 14,
             compiler_params=pltpu.CompilerParams(collective_id=0, has_side_effects=True, vmem_limit_bytes=38 * 2**20),
             name="exchange",
@@ -407,8 +417,9 @@
             out_shape=(jax.ShapeDtypeStruct((n_draft, seqs, vocab), F32), jax.ShapeDtypeStruct((seqs, vocab), F32),
                        jax.ShapeDtypeStruct((n_draft, seqs), F32), jax.ShapeDtypeStruct((1, seqs), F32)),
             in_specs=[vmem_spec] * 4,
-            out_specs=(any_spec, any_spec, vmem_spec, vmem_spec),
-            scratch_shapes=[pltpu.VMEM((SLOTS, seqs // 2, vocab), F32), dma((SLOTS,)), dma],
+            out_specs=(any_spec,) * 4,
+            scratch_shapes=[pltpu.VMEM((SLOTS, seqs // 2, vocab), F32), pltpu.VMEM((n_draft, seqs), F32),
+                            pltpu.VMEM((1, seqs), F32), dma((SLOTS,)), dma, dma((2,))],
             compiler_params=pltpu.CompilerParams(vmem_limit_bytes=12 * 2**20),
             name="output",
         )(ex, bonus, early, late)

time: 427 us -> 426 us (level)
  no operation moved by 1% of the time
where the time goes in v4:
time: 426 us
  Pallas kernels  425 us (100%)
    pallas_call x1, Pallas kernels, local_step(): pl.pallas_call(functools.partial(exchange_kernel, dims), out_shape=(pltpu...  417 us

profile of v4, /device:TPU:0, one launch (start us, length us, event | category | flops | bytes accessed | tf_op | source)
XLA Modules:
  0.0 425.6 jit_solution(17501922841949115602)
XLA Ops:
  0.6 417.5 %exchange.1 = (f32[6,256,3072]{2,1,0:T(8,128)S(1)}, f32[256,3072]{1,0:T(8,128)S(1)}, f32[4,8,128]{2,1,0:T(8,128)S(1)}, f32[16,2,256]{2,1,0:T(2,128)S(1)}) custom-call(bf16[7,256,2048]{2,1,0:T(8,128)(2,1)} %bitcast.7, bf16[2048,3072]{1,0:T(8,128)(2,1)} %w_ref.1, f32[6,16,49152]{2,1,0:T(8,128)} %bitcast.6, s32[6,256]{1,0:T(8,128)} %bitcast.8), custom_call_target="tpu_custom_call" | custom-call | tf_op jit(solution)/shard_map/exchange/pallas_call | solution.py:397
  418.1 7.5 %output.1 = (f32[6,256,3072]{2,1,0:T(8,128)}, f32[256,3072]{1,0:T(8,128)}, f32[6,256]{1,0:T(8,128)}, f32[1,256]{1,0:T(1,128)}) custom-call(f32[6,256,3072]{2,1,0:T(8,128)S(1)} %get-tuple-element.12.ex_ref, f32[256,3072]{1,0:T(8,128)S(1)} %get-tuple-element.13.bonus_ref, f32[4,8,128]{2,1,0:T(8,128)S(1)} %get-tuple-element.14.early_ref, ...), custom_call_target="tpu_custom_call" | custom-call | tf_op jit(solution)/shard_map/output/pallas_call | solution.py:415

commit v5 on v4

--- a/solution.py
+++ b/solution.py
@@ -13,6 +13,7 @@
 F32 = jnp.float32
 SEND = ((3, 3, 0, 0), (1, 0, 3, 2), (2, 2, 1, 1))
 RECV = ((3, 0, 3, 0), (2, 3, 0, 1), (1, 2, 1, 2))
+LAST_RECV = ((1, 0, 3, 2), (2, 3, 0, 1))
 CORE_OFFSETS = (0, 2, 1, 3)
 NT = 512
 
@@ -49,9 +50,9 @@
     return jnp.sum(jnp.where(lanes(row.shape[1], first, rows), row, 0.0), axis=1, keepdims=True)
 
 
-def exchange_kernel(dims, hid_ref, w_ref, q_ref, x_ref, ex_ref, bonus_ref, early_ref, late_ref,
-                    hid_v, w_v, z_v, x_v, tok_v, stat_out, stat_1, stat_2, norm_v, sum_out, sum_1, sum_2, hid_sem, w_sem, own_sem, x_sem,
-                    q_send, q_recv, r_recv, l_send, l_recv,
+def exchange_kernel(dims, hid_ref, w_ref, q_ref, x_ref, ex_ref, bonus_ref, early_ref, late_ref, part_p_ref, part_q_ref, part_head_ref, part_tok_ref,
+                    hid_v, w_v, z_v, x_v, tok_v, stat_out, stat_1, stat_2, norm_v, sum_out, sum_1, sum_2, hid_sem, w_sem, own_sem, x_sem, part_sem,
+                    q_send, q_recv, r_send, r_recv, h_send, h_recv,
                     a1_send, a1_recv, a2_send, a2_recv, a3_send, a3_recv, b1_send, b1_recv, b2_send, b2_recv, b3_send, b3_recv):
     n_pos, seqs, depth, vocab, n_loc, na, nb = dims
     n_draft = n_pos - 1
@@ -62,38 +63,38 @@
     dp, za, tb = lax.axis_index("dp"), lax.axis_index("tpa"), lax.axis_index("tpb")
     me = za * nb + tb
 
-    def send_peer(k):
-        inner = (za == 1) | (za == 2)
-        if k < 3:
-            end, mid = (pick(za, SEND[0]), CORE_OFFSETS[k]), (za, k + 1)
-        else:
-            mid = (pick(za, SEND[(k - 3) // nb]), CORE_OFFSETS[(k - 3) % nb])
-            end = (pick(za, SEND[k // nb]), CORE_OFFSETS[k % nb]) if k < 12 else (za, k - 11)
-        plane = jnp.where(inner, mid[0], end[0])
-        return plane, lax.rem(tb + jnp.where(inner, mid[1], end[1]), nb)
+    inner = (za == 1) | (za == 2)
+
+    def choose(end, mid):
+        return [(jnp.where(inner, m[0], e[0]), lax.rem(tb + jnp.where(inner, m[1], e[1]), nb)) for e, m in zip(end, mid)]
+
+    own = [(za, k) for k in range(1, nb)]
+    steps = [[(pick(za, SEND[step]), CORE_OFFSETS[k]) for k in range(nb)] for step in range(3)]
+    first_order = choose(steps[0] + steps[1] + steps[2] + own, own + steps[0] + steps[1] + steps[2])
+    last_order = choose(steps[1] + own + steps[2] + steps[0], own + steps[1] + steps[0] + steps[2])
 
     def recv_peer(k):
         step, off = (k - 3) // nb, lax.rem(jnp.int32(k) + 1, nb)
-        plane = jnp.where(k < 3, za, jnp.where(step == 0, pick(za, RECV[0]),
-                          jnp.where(step == 1, pick(za, RECV[1]), pick(za, RECV[2]))))
+        plane = jnp.where(k < 3, za, jnp.where(step == 0, pick(za, LAST_RECV[0]),
+                          jnp.where(step == 1, pick(za, LAST_RECV[1]), na - 1 - za)))
         off = jnp.where(k < 3, k + 1, nb - pick(off, CORE_OFFSETS))
         return plane, lax.rem(tb + off, nb)
 
     def rows_of(group):
         return pl.ds(pl.multiple_of(group * n_loc, 8), n_loc)
 
-    def q_copy(part, plane, core, own_group, column):
+    def q_copy(part, plane, core, own_group, column, send=q_send):
         i0, ni = (0, n_early) if part == 0 else (n_early, 1)
         recv = q_recv.at[own_group // nb] if part == 0 else r_recv.at[own_group]
         return pltpu.make_async_remote_copy(
             src_ref=q_ref.at[pl.ds(i0, ni), :, pl.ds(pl.multiple_of(column * vocab, 128), vocab)],
             dst_ref=ex_ref.at[pl.ds(i0, ni), rows_of(own_group), :],
-            send_sem=q_send, recv_sem=recv,
+            send_sem=send, recv_sem=recv,
             device_id=(dp, plane, core), device_id_type=MESH)
 
     def q_to(part, k):
-        plane, core = send_peer(k)
-        return q_copy(part, plane, core, me, plane * nb + core)
+        plane, core = (first_order, last_order)[part][k]
+        return q_copy(part, plane, core, me, plane * nb + core, r_send if (part, k) >= (1, 11) else q_send)
 
     def q_from_plane(plane, count):
         rows = ex_ref.at[pl.ds(0, n_early), pl.ds(0, count * n_loc), :]
@@ -118,10 +119,6 @@
     def across(ref, send, recv):
         planes = [lax.rem(za + k, na) for k in range(1, na)]
         return [small(ref, ref, send, recv, za, za, plane, tb) for plane in planes]
-
-    def late_to(k):
-        plane, core = send_peer(k)
-        return small(late_ref, late_ref, l_send, l_recv, me, me, plane, core)
 
     def start(copies):
         for copy in copies:
@@ -147,6 +144,9 @@
         return pltpu.make_async_copy(w_ref.at[:, pl.ds(pl.multiple_of(tile * NT, NT), NT)], w_v.at[slot], w_sem.at[slot])
 
     hid_copy = pltpu.make_async_copy(hid_ref, hid_v, hid_sem)
+    part_copies = [pltpu.make_async_copy(
+        q_ref.at[n_early, :, pl.ds(pl.multiple_of(((na - 1 - za) * nb + core) * vocab, 128), vocab)],
+        part_q_ref.at[pl.ds(core * n_loc, n_loc), :], part_sem.at[core]) for core in range(nb)]
     x_copy = pltpu.make_async_copy(x_ref, x_v, x_sem)
     own_copy = pltpu.make_async_copy(
         q_ref.at[:, :, pl.ds(pl.multiple_of(me * vocab, 128), vocab)], ex_ref.at[:, rows_of(me), :], own_sem)
@@ -160,6 +160,8 @@
     for k in range(4):
         q_to(0, k).start()
     x_copy.start()
+    for copy in part_copies:
+        copy.start()
     hid_copy.start()
     w_copy(0, 0).start()
     own_copy.start()
@@ -169,6 +171,8 @@
     for i in range(n_draft):
         tok_v[i] = jnp.broadcast_to(to_col(tok_rows[i:i + 1]), (seqs, 128)).astype(jnp.int32) - me * vocab
     hid_copy.wait()
+    for copy in part_copies:
+        copy.wait()
 
     @pl.loop(0, n_tiles)
     def _(tile):
@@ -212,8 +216,13 @@
     start(in_plane(norm_v, norm_v, a3_send, a3_recv, False))
     for k in range(6, 15):
         q_to(0, k).start()
-    for k in range(11):
+    for k in range(10):
         q_to(1, k).start()
+
+    @pl.when(jnp.logical_not(inner))
+    def _():
+        q_to(1, 10).start()
+
     await_slots(norm_v, a3_recv, 3)
 
     def probs(i, group):
@@ -267,85 +276,195 @@
 
     sum_1[tb] = sum_out[tb]
     start(in_plane(sum_out, sum_1, b1_send, b1_recv, True))
-    for k in (11, 12):
-        q_to(1, k).start()
     await_slots(sum_1, b1_recv, 3)
     sum_2[za] = add(sum_1)
     start(across(sum_2, b2_send, b2_recv))
-    for k in (13, 14):
-        q_to(1, k).start()
-
-    def absorb_late(group, rows):
+
+    partner = na - 1 - za
+    head = pltpu.make_async_remote_copy(
+        src_ref=q_ref.at[n_early, pl.ds(0, n_loc // 2), pl.ds(pl.multiple_of((partner * nb + tb) * vocab, 128), vocab)],
+        dst_ref=part_head_ref, send_sem=h_send, recv_sem=h_recv, device_id=(dp, partner, tb), device_id_type=MESH)
+
+    @pl.when(inner)
+    def _():
+        q_to(1, 10).start()
+        head.start()
+
+    @pl.loop(0, nb)
+    def _(core):
+        group = partner * nb + core
+        part_p_ref[pl.ds(pl.multiple_of(core * n_loc, 8), n_loc), :] = probs(n_early, group)
+        part_tok_ref[pl.ds(pl.multiple_of(core * n_loc, 8), n_loc), :] = tok_v[n_early, rows_of(group), :]
+
+    def absorb_late(group):
         z, a = cell(n_early, group)
-        return rows[0] + spread(z, seqs, group * n_loc), rows[1] + spread(a, seqs, group * n_loc)
-
-    def arrived(k, rows):
+        late_ref[...] += jnp.concatenate([spread(z, seqs, group * n_loc), spread(a, seqs, group * n_loc)], axis=0)
+
+    def arrived(k):
         plane, core = recv_peer(k)
         q_from(plane * nb + core).wait_recv()
-        return absorb_late(plane * nb + core, rows)
-
-    zero = jnp.zeros((1, seqs), F32)
-    rows = lax.fori_loop(0, 11, arrived, absorb_late(me, (zero, zero)))
+        absorb_late(plane * nb + core)
+
+    late_ref[...] = jnp.zeros_like(late_ref)
+    absorb_late(me)
+    pl.loop(0, 10)(arrived)
+
+    plane, core = recv_peer(10)
+    q_from(plane * nb + core).wait_recv()
+
+    @pl.when(jnp.logical_not(inner))
+    def _():
+        for k in range(11, 15):
+            q_to(1, k).start()
+
+    absorb_late(plane * nb + core)
     await_slots(sum_2, b2_recv, 3)
     early_ref[tb] = add(sum_2)
     start(in_plane(early_ref, early_ref, b3_send, b3_recv, False))
-    rows = lax.fori_loop(11, 15, arrived, rows)
-
-    late_ref[me] = jnp.concatenate(rows, axis=0)
-    sent = q_ref.at[:, :, pl.ds(0, (n_peers - 1) * vocab)]
+
+    @pl.when(inner)
+    def _():
+        head.wait()
+
+    @pl.when(jnp.logical_not(inner))
+    def _():
+        pl.loop(11, 15)(arrived)
+        sent = q_ref.at[0:4, :, pl.ds(0, vocab)]
+        pltpu.make_async_copy(sent, sent, r_send).wait()
+
+    await_slots(early_ref, b3_recv, 3)
+    slices = (n_peers - 1) * n_early + 11
+    sent = q_ref.at[:, :, pl.ds(0, slices * vocab // n_draft)]
     pltpu.make_async_copy(sent, sent, q_send).wait()
-    for k in others:
-        late_to(k).start()
-    await_slots(early_ref, b3_recv, 3)
-    await_slots(late_ref, l_recv, n_peers - 1)
-    await_slots(late_ref, l_send, n_peers - 1)
     for ref, sem in ((stat_1, a1_send), (stat_2, a2_send), (norm_v, a3_send), (sum_1, b1_send), (sum_2, b2_send),
                      (early_ref, b3_send)):
         await_slots(ref, sem, 3)
 
 
+def last_kernel(dims, q_ref, head_ref, p_ref, tok_ref, part_ref, order_ref, ex_ref, late_ref, own_v, ready, q_send, q_recv, l_send, l_recv):
+    n_draft, seqs, vocab, n_loc, na, nb = dims
+    n_peers = na * nb
+    dp, za, tb = lax.axis_index("dp"), lax.axis_index("tpa"), lax.axis_index("tpb")
+    me, partner = za * nb + tb, na - 1 - za
+    inner = (za == 1) | (za == 2)
+    same = [(za, lax.rem(tb + k, nb)) for k in range(1, nb)] + [(partner, lax.rem(tb + k, nb)) for k in range(nb)]
+    other_planes = (jnp.where(inner, 0, 1), jnp.where(inner, 3, 2))
+    other = [(plane, lax.rem(tb + k, nb)) for plane in other_planes for k in range(nb)]
+
+    def signal(sem, peers):
+        for plane, core in peers:
+            pl.semaphore_signal(sem, inc=1, device_id=(dp, plane, core), device_id_type=MESH)
+
+    barrier = pltpu.get_barrier_semaphore()
+    signal(barrier, same)
+
+    @pl.when(inner)
+    def _():
+        signal(barrier, other)
+
+    pl.semaphore_wait(barrier, jnp.where(inner, 2 * nb - 1, n_peers - 1))
+
+    @pl.when(jnp.logical_not(inner))
+    def _():
+        signal(ready, other)
+
+    def q_copy(core, own_core, first):
+        return pltpu.make_async_remote_copy(
+            src_ref=q_ref.at[pl.ds(pl.multiple_of(core * n_loc + first, 8), n_loc - first), :],
+            dst_ref=ex_ref.at[pl.ds(pl.multiple_of(own_core * n_loc + first, 8), n_loc - first), :],
+            send_sem=q_send, recv_sem=q_recv.at[own_core], device_id=(dp, partner, core), device_id_type=MESH)
+
+    def late_to(peer):
+        plane, core = peer
+        return pltpu.make_async_remote_copy(
+            src_ref=late_ref.at[me], dst_ref=late_ref.at[me], send_sem=l_send, recv_sem=l_recv,
+            device_id=(dp, plane, core), device_id_type=MESH)
+
+    own_v[...] = part_ref[...]
+
+    @pl.when(inner)
+    def _():
+        for k in CORE_OFFSETS:
+            q_copy(lax.rem(tb + k, nb), tb, 0 if k else n_loc // 2).start()
+
+        ex_ref[pl.ds(pl.multiple_of(tb * n_loc, 8), n_loc // 2), :] = head_ref[...]
+        q_copy(tb, tb, n_loc // 2).wait_recv()
+
+        @pl.loop(0, nb)
+        def _(k):
+            core = lax.rem(tb + nb - pick(k, CORE_OFFSETS), nb)
+            rows = pl.ds(pl.multiple_of(core * n_loc, 8), n_loc)
+
+            @pl.when(k > 0)
+            def _():
+                q_copy(core, core, 0).wait_recv()
+
+            p, q, tok = p_ref[rows, :], ex_ref[rows, :], tok_ref[rows, 0:1]
+            hit = lax.broadcasted_iota(jnp.int32, (n_loc, vocab), 1) == tok
+            excess = jnp.maximum(p - q, 0.0)
+            ex_ref[rows, :] = excess
+            z = jnp.sum(excess, axis=1, keepdims=True)
+            p_pick = jnp.sum(jnp.where(hit, p, 0.0), axis=1, keepdims=True)
+            q_pick = jnp.sum(jnp.where(hit, q, 0.0), axis=1, keepdims=True)
+            owned = (tok >= 0) & (tok < vocab)
+            a = jnp.where(owned, jnp.minimum(1.0, p_pick / jnp.where(owned, q_pick, 1.0)), 0.0)
+            first = (partner * nb + core) * n_loc
+            own_v[...] += jnp.concatenate([spread(z, seqs, first), spread(a, seqs, first)], axis=0)
+
+    late_ref[me] = own_v[...]
+
+    @pl.when(inner)
+    def _():
+        sent = q_ref.at[pl.ds(0, nb * n_loc - n_loc // 2), :]
+        pltpu.make_async_copy(sent, sent, q_send).wait()
+        pl.semaphore_wait(ready, 2 * nb)
+
+    for peer in other + same:
+        late_to(peer).start()
+    slots = late_ref.at[pl.ds(0, n_peers - 1)]
+    pltpu.make_async_copy(slots, slots, l_recv).wait()
+    pltpu.make_async_copy(slots, slots, l_send).wait()
+
+
 SLOTS = 4
 
 
-def output_kernel(na, nb, ex_ref, bonus_ref, early_ref, late_ref, res_ref, bonus_out, accept_ref, expected_ref,
-                  stage, accept_v, expected_v, stage_sem, bonus_sem, small_sem):
-    n_draft, seqs, vocab = ex_ref.shape
+def by_position(na, nb, early_ref, which, n_early, seqs):
     n_peers = na * nb
-    n_loc, half = seqs // n_peers, seqs // 2
-    bonus_copy = pltpu.make_async_copy(bonus_ref, bonus_out, bonus_sem)
-    bonus_copy.start()
-
-    late = late_ref[0]
-    for k in range(1, n_peers):
-        late += late_ref[k]
+    n_loc = seqs // n_peers
     lane = lax.broadcasted_iota(jnp.int32, (n_peers, 128), 1)
     mine = (lax.broadcasted_iota(jnp.int32, (n_peers, seqs), 1) // n_loc
             == lax.broadcasted_iota(jnp.int32, (n_peers, seqs), 0))
-
-    def by_position(which):
-        table = jnp.concatenate(
-            [early_ref[g % nb, na * which + g // nb:na * which + g // nb + 1, :] for g in range(n_peers)], axis=0)
-        out = jnp.broadcast_to(late[which:which + 1], (8, seqs))
-        for i in range(n_draft - 1):
-            x = pltpu.roll(table, (128 - n_loc * i) % 128, 1)
-            x = jnp.where(lane < n_loc, x, 0.0)
-            shift = n_loc
-            while shift < 128:
-                x = x + pltpu.roll(x, shift, 1)
-                shift *= 2
-            x = jnp.concatenate([x] * (seqs // 128), axis=1)
-            row = jnp.sum(jnp.where(mine, x, 0.0), axis=0, keepdims=True)
-            out = jnp.where(lax.broadcasted_iota(jnp.int32, (8, seqs), 0) == i, row, out)
-        return out
-
-    inv = 1.0 / by_position(0)
+    table = jnp.concatenate(
+        [early_ref[g % nb, na * which + g // nb:na * which + g // nb + 1, :] for g in range(n_peers)], axis=0)
+    out = jnp.ones((8, seqs), F32)
+    for i in range(n_early):
+        x = pltpu.roll(table, (128 - n_loc * i) % 128, 1)
+        x = jnp.where(lane < n_loc, x, 0.0)
+        shift = n_loc
+        while shift < 128:
+            x = x + pltpu.roll(x, shift, 1)
+            shift *= 2
+        x = jnp.concatenate([x] * (seqs // 128), axis=1)
+        row = jnp.sum(jnp.where(mine, x, 0.0), axis=0, keepdims=True)
+        out = jnp.where(lax.broadcasted_iota(jnp.int32, (8, seqs), 0) == i, row, out)
+    return out
+
+
+def early_output_kernel(na, nb, ex_ref, bonus_ref, early_ref, res_ref, bonus_out, order_ref, stage, stage_sem, bonus_sem):
+    n_draft, seqs, vocab = ex_ref.shape
+    n_early, half = n_draft - 1, seqs // 2
+    bonus_copy = pltpu.make_async_copy(bonus_ref, bonus_out, bonus_sem)
+    bonus_copy.start()
+    order_ref[...] = jnp.zeros_like(order_ref)
+    inv = 1.0 / by_position(na, nb, early_ref, 0, n_early, seqs)
 
     def out_copy(k, slot):
         i, h = k // 2, lax.rem(k, 2)
         return pltpu.make_async_copy(
             stage.at[slot], res_ref.at[i, pl.ds(pl.multiple_of(h * half, half), half), :], stage_sem.at[slot])
 
-    @pl.loop(0, 2 * n_draft)
+    @pl.loop(0, 2 * n_early)
     def _(k):
         i, h, slot = k // 2, lax.rem(k, 2), lax.rem(k, SLOTS)
         row = get_row(inv, i)
@@ -362,7 +481,48 @@
 
         out_copy(k, slot).start()
 
-    accept = by_position(1)[:n_draft]
+    for k in range(2 * n_early - SLOTS, 2 * n_early):
+        out_copy(k, k % SLOTS).wait()
+    bonus_copy.wait()
+
+
+def late_output_kernel(na, nb, ex_ref, part_ref, early_ref, late_ref, res_in, res_ref, accept_ref, expected_ref,
+                       stage, accept_v, expected_v, stage_sem, small_sem):
+    n_draft, seqs, vocab = ex_ref.shape
+    n_early, block = n_draft - 1, seqs // na
+    za = lax.axis_index("tpa")
+    inner, partner = (za == 1) | (za == 2), na - 1 - za
+    late = late_ref[0]
+    for k in range(1, na * nb):
+        late += late_ref[k]
+    col = to_col(1.0 / late[0:1])
+
+    def out_copy(plane):
+        rows = pl.ds(plane * block, block)
+        return pltpu.make_async_copy(stage.at[rows], res_ref.at[n_early, rows, :], stage_sem.at[plane])
+
+    for plane in range(na):
+        rows, scale = pl.ds(plane * block, block), col[plane * block:(plane + 1) * block]
+        from_part = inner & (partner == plane)
+
+        @pl.when(from_part)
+        def _():
+            @pl.loop(0, vocab // NT)
+            def _(t):
+                cols = pl.ds(pl.multiple_of(t * NT, NT), NT)
+                stage[rows, cols] = part_ref[:, cols] * scale
+
+        @pl.when(jnp.logical_not(from_part))
+        def _():
+            @pl.loop(0, vocab // NT)
+            def _(t):
+                cols = pl.ds(pl.multiple_of(t * NT, NT), NT)
+                stage[rows, cols] = ex_ref[n_early, rows, cols] * scale
+
+        out_copy(plane).start()
+
+    accept = by_position(na, nb, early_ref, 1, n_early, seqs)
+    accept = jnp.where(lax.broadcasted_iota(jnp.int32, accept.shape, 0) == n_early, late[1:2], accept)[:n_draft]
     accept_v[...] = accept
     prod = accept[0:1]
     expected = prod
@@ -374,9 +534,8 @@
                     pltpu.make_async_copy(expected_v, expected_ref, small_sem.at[1]))
     for copy in small_copies:
         copy.start()
-    for k in range(2 * n_draft - SLOTS, 2 * n_draft):
-        out_copy(k, k % SLOTS).wait()
-    bonus_copy.wait()
+    for plane in range(na):
+        out_copy(plane).wait()
     for copy in small_copies:
         copy.wait()
 
@@ -394,12 +553,15 @@
         dims = (n_pos, seqs, depth, vocab, n_loc, na, nb)
         dma = pltpu.SemaphoreType.DMA
         small = pltpu.VMEM((4, 8, 128), F32)
-        ex, bonus, early, late = pl.pallas_call(
+        q_rows = q_draft.transpose(1, 0, 2)
+        block = seqs // na
+        ex, bonus, early, late_part, part_p, part_q, part_head, part_tok = pl.pallas_call(
             functools.partial(exchange_kernel, dims),
-            out_shape=(pltpu.VMEM((n_draft, seqs, vocab), F32), pltpu.VMEM((seqs, vocab), F32),
-                       small, pltpu.VMEM((n_peers, 2, seqs), F32)),
+            out_shape=(pltpu.VMEM((n_draft, seqs, vocab), F32), pltpu.VMEM((seqs, vocab), F32), small,
+                       pltpu.VMEM((2, seqs), F32), pltpu.VMEM((block, vocab), F32), pltpu.VMEM((block, vocab), F32),
+                       pltpu.VMEM((n_loc // 2, vocab), F32), pltpu.VMEM((block, 128), jnp.int32)),
             in_specs=[any_spec] * 4,
-            out_specs=(vmem_spec,) * 4,
+            out_specs=(vmem_spec,) * 8,
             scratch_shapes=[
                 pltpu.VMEM((n_pos, seqs, depth), jnp.bfloat16),
                 pltpu.VMEM((2, depth, NT), jnp.bfloat16),
@@ -407,22 +569,42 @@
                 pltpu.VMEM((n_draft, seqs), jnp.int32),
                 pltpu.VMEM((n_draft, seqs, 128), jnp.int32),
                 small, small, small, small, small, small, small,
-                dma, dma((2,)), dma, dma, dma, dma((na,)), dma((n_peers,)),
+                dma, dma((2,)), dma, dma, dma((nb,)), dma, dma((na,)), dma, dma((n_peers,)),
             ] + [dma] * 14,
             compiler_params=pltpu.CompilerParams(collective_id=0, has_side_effects=True, vmem_limit_bytes=38 * 2**20),
             name="exchange",
-        )(hidden.transpose(1, 0, 2), w_head, q_draft.transpose(1, 0, 2), x_draft.T)
-        res, bonus_out, accept, expected = pl.pallas_call(
-            functools.partial(output_kernel, na, nb),
+        )(hidden.transpose(1, 0, 2), w_head, q_rows, x_draft.T)
+        res, bonus_out, order = pl.pallas_call(
+            functools.partial(early_output_kernel, na, nb),
             out_shape=(jax.ShapeDtypeStruct((n_draft, seqs, vocab), F32), jax.ShapeDtypeStruct((seqs, vocab), F32),
-                       jax.ShapeDtypeStruct((n_draft, seqs), F32), jax.ShapeDtypeStruct((1, seqs), F32)),
-            in_specs=[vmem_spec] * 4,
-            out_specs=(any_spec,) * 4,
-            scratch_shapes=[pltpu.VMEM((SLOTS, seqs // 2, vocab), F32), pltpu.VMEM((n_draft, seqs), F32),
-                            pltpu.VMEM((1, seqs), F32), dma((SLOTS,)), dma, dma((2,))],
+                       pltpu.VMEM((8, 128), F32)),
+            in_specs=[vmem_spec] * 3,
+            out_specs=(any_spec, any_spec, vmem_spec),
+            scratch_shapes=[pltpu.VMEM((SLOTS, seqs // 2, vocab), F32), dma((SLOTS,)), dma],
             compiler_params=pltpu.CompilerParams(vmem_limit_bytes=12 * 2**20),
-            name="output",
-        )(ex, bonus, early, late)
+            name="early_output",
+        )(ex, bonus, early)
+        part, late = pl.pallas_call(
+            functools.partial(last_kernel, (n_draft, seqs, vocab, n_loc, na, nb)),
+            out_shape=(pltpu.VMEM((block, vocab), F32), pltpu.VMEM((n_peers, 2, seqs), F32)),
+            in_specs=[vmem_spec] * 6,
+            out_specs=(vmem_spec, vmem_spec),
+            scratch_shapes=[pltpu.VMEM((2, seqs), F32), pltpu.SemaphoreType.REGULAR, dma, dma((nb,)), dma, dma],
+            compiler_params=pltpu.CompilerParams(collective_id=1, has_side_effects=True, vmem_limit_bytes=28 * 2**20),
+            name="last",
+        )(part_q, part_head, part_p, part_tok, late_part, order)
+        res, accept, expected = pl.pallas_call(
+            functools.partial(late_output_kernel, na, nb),
+            out_shape=(jax.ShapeDtypeStruct((n_draft, seqs, vocab), F32), jax.ShapeDtypeStruct((n_draft, seqs), F32),
+                       jax.ShapeDtypeStruct((1, seqs), F32)),
+            in_specs=[vmem_spec] * 4 + [any_spec],
+            out_specs=(any_spec,) * 3,
+            scratch_shapes=[pltpu.VMEM((seqs, vocab), F32), pltpu.VMEM((n_draft, seqs), F32), pltpu.VMEM((1, seqs), F32),
+                            dma((na,)), dma((2,))],
+            input_output_aliases={4: 0},
+            compiler_params=pltpu.CompilerParams(vmem_limit_bytes=12 * 2**20),
+            name="late_output",
+        )(ex, part, early, late, res)
         return accept.T, expected.reshape(seqs), res.transpose(1, 0, 2), bonus_out
 
     return jax.shard_map(

time: 426 us -> 420 us (0.986)
  Pallas kernels: 425 us -> 419 us
    pallas_call x1, Pallas kernels: 417 us -> 401 us  [local_step(): pl.pallas_call(functools.partial(exchange_kernel, dims), out_shape=(pltpu...]
    pallas_call x1 -> x3, Pallas kernels: 7.49 us -> 18.5 us  [the longest x1 10.1 us: local_step(): pl.pallas_call(functools.partial(last_kernel, (n_draft, seqs, vocab, n_lo...]
where the time goes in v5:
time: 420 us
  Pallas kernels  419 us (100%)
    pallas_call x1, Pallas kernels, local_step(): pl.pallas_call(functools.partial(exchange_kernel, dims), out_shape=(pltpu...  401 us
    pallas_call x1, Pallas kernels, local_step(): pl.pallas_call(functools.partial(last_kernel, (n_draft, seqs, vocab, n_lo...  10.1 us

profile of v5, /device:TPU:0, one launch (start us, length us, event | category | flops | bytes accessed | tf_op | source)
XLA Modules:
  0.0 420.1 jit_solution(6532877463916407534)
XLA Ops:
  0.6 400.9 %exchange.1 = (f32[6,256,3072]{2,1,0:T(8,128)S(1)}, f32[256,3072]{1,0:T(8,128)S(1)}, f32[4,8,128]{2,1,0:T(8,128)S(1)}, f32[2,256]{1,0:T(2,128)S(1)}, f32[64,3072...) custom-call(bf16[7,256,2048]{2,1,0:T(8,128)(2,1)} %bitcast.8, ...), custom_call_target="tpu_custom_call" | custom-call | tf_op jit(solution)/shard_map/exchange/pallas_call | solution.py:558
  401.5 6.5 %early_output.1 = (f32[6,256,3072]{2,1,0:T(8,128)}, f32[256,3072]{1,0:T(8,128)}, f32[8,128]{1,0:T(8,128)S(1)}) custom-call(f32[6,256,3072]{2,1,0:T(8,128)S(1)} %get-tuple-element.20.ex_ref, f32[256,3072]{1,0:T(8,128)S(1)} %get-tuple-element.26.bonus_ref, f32[4,8,128]{2,1,0:T(8,128)S(1)} %get-tuple-element.27.early_ref), custom_call_target="tpu_custom_call" | custom-call | tf_op jit(solution)/shard_map/early_output/pallas_call | solution.py:577
  408.1 10.1 %last.1 = (f32[64,3072]{1,0:T(8,128)S(1)}, f32[16,2,256]{2,1,0:T(2,128)S(1)}) custom-call(f32[64,3072]{1,0:T(8,128)S(1)} %get-tuple-element.21.q_ref, f32[8,3072]{1,0:T(8,128)S(1)} %get-tuple-element.22.head_ref, f32[64,3072]{1,0:T(8,128)S(1)} %get-tuple-element.23.p_ref, s32[64,128]{1,0:T(8,128)S(1)} %get-tuple-element.24.tok_ref, ...), custom_call_target="tpu_custom_call" | custom-call | tf_op jit(solution)/shard_map/last/pallas_call | solution.py:587
  418.2 1.9 late_output.1

commit v6 on v5

--- a/solution.py
+++ b/solution.py
@@ -52,7 +52,7 @@
 
 def exchange_kernel(dims, hid_ref, w_ref, q_ref, x_ref, ex_ref, bonus_ref, early_ref, late_ref, part_p_ref, part_q_ref, part_head_ref, part_tok_ref,
                     hid_v, w_v, z_v, x_v, tok_v, stat_out, stat_1, stat_2, norm_v, sum_out, sum_1, sum_2, hid_sem, w_sem, own_sem, x_sem, part_sem,
-                    q_send, q_recv, r_send, r_recv, h_send, h_recv,
+                    ready, q_send, q_recv, r_send, r_recv, h_send, h_recv,
                     a1_send, a1_recv, a2_send, a2_recv, a3_send, a3_recv, b1_send, b1_recv, b2_send, b2_recv, b3_send, b3_recv):
     n_pos, seqs, depth, vocab, n_loc, na, nb = dims
     n_draft = n_pos - 1
@@ -70,7 +70,7 @@
 
     own = [(za, k) for k in range(1, nb)]
     steps = [[(pick(za, SEND[step]), CORE_OFFSETS[k]) for k in range(nb)] for step in range(3)]
-    first_order = choose(steps[0] + steps[1] + steps[2] + own, own + steps[0] + steps[1] + steps[2])
+    first_order = choose(steps[0] + steps[1] + steps[2] + own, steps[2][:1] + own + steps[0] + steps[1] + steps[2][1:])
     last_order = choose(steps[1] + own + steps[2] + steps[0], own + steps[1] + steps[0] + steps[2])
 
     def recv_peer(k):
@@ -151,20 +151,47 @@
     own_copy = pltpu.make_async_copy(
         q_ref.at[:, :, pl.ds(pl.multiple_of(me * vocab, 128), vocab)], ex_ref.at[:, rows_of(me), :], own_sem)
 
+    def signal(sem, peers):
+        for plane, core in peers:
+            pl.semaphore_signal(sem, inc=1, device_id=(dp, plane, core), device_id_type=MESH)
+
+    partner = na - 1 - za
+    own_plane = [(za, lax.rem(tb + k, nb)) for k in range(1, nb)]
+    partner_plane = [(partner, lax.rem(tb + k, nb)) for k in range(nb)]
+    other_planes = [(plane, lax.rem(tb + k, nb)) for plane in (jnp.where(inner, 0, 1), jnp.where(inner, 3, 2)) for k in range(nb)]
+
     barrier = pltpu.get_barrier_semaphore()
-    for k in range(1, n_peers):
-        pl.semaphore_signal(barrier, inc=1, device_id=(dp, lax.rem(za + k // nb, na), lax.rem(tb + k % nb, nb)),
-                            device_id_type=MESH)
-    pl.semaphore_wait(barrier, n_peers - 1)
-
-    for k in range(4):
-        q_to(0, k).start()
+    signal(barrier, partner_plane)
+
+    @pl.when(inner)
+    def _():
+        signal(barrier, other_planes)
+
+    @pl.when(jnp.logical_not(inner))
+    def _():
+        signal(barrier, own_plane)
+
+    pl.semaphore_wait(barrier, jnp.where(inner, nb, n_peers - 1))
+    q_to(0, 0).start()
+
+    @pl.when(jnp.logical_not(inner))
+    def _():
+        for k in range(1, 4):
+            q_to(0, k).start()
+        signal(ready, other_planes)
+
     x_copy.start()
     for copy in part_copies:
         copy.start()
     hid_copy.start()
     w_copy(0, 0).start()
     own_copy.start()
+
+    @pl.when(inner)
+    def _():
+        pl.semaphore_wait(ready, 2 * nb)
+        for k in range(1, 4):
+            q_to(0, k).start()
 
     x_copy.wait()
     tok_rows = x_v[...].astype(F32)
@@ -280,7 +307,6 @@
     sum_2[za] = add(sum_1)
     start(across(sum_2, b2_send, b2_recv))
 
-    partner = na - 1 - za
     head = pltpu.make_async_remote_copy(
         src_ref=q_ref.at[n_early, pl.ds(0, n_loc // 2), pl.ds(pl.multiple_of((partner * nb + tb) * vocab, 128), vocab)],
         dst_ref=part_head_ref, send_sem=h_send, recv_sem=h_recv, device_id=(dp, partner, tb), device_id_type=MESH)
@@ -569,7 +595,7 @@
                 pltpu.VMEM((n_draft, seqs), jnp.int32),
                 pltpu.VMEM((n_draft, seqs, 128), jnp.int32),
                 small, small, small, small, small, small, small,
-                dma, dma((2,)), dma, dma, dma((nb,)), dma, dma((na,)), dma, dma((n_peers,)),
+                dma, dma((2,)), dma, dma, dma((nb,)), pltpu.SemaphoreType.REGULAR, dma, dma((na,)), dma, dma((n_peers,)),
             ] + [dma] * 14,
             compiler_params=pltpu.CompilerParams(collective_id=0, has_side_effects=True, vmem_limit_bytes=38 * 2**20),
             name="exchange",

time: 420 us -> 419 us (level)
  no operation moved by 1% of the time
where the time goes in v6:
time: 419 us
  Pallas kernels  418 us (100%)
    pallas_call x1, Pallas kernels, local_step(): pl.pallas_call(functools.partial(exchange_kernel, dims), out_shape=(pltpu...  399 us
    pallas_call x1, Pallas kernels, local_step(): pl.pallas_call(functools.partial(last_kernel, (n_draft, seqs, vocab, n_lo...  10.1 us

profile of v6, /device:TPU:0, one launch (start us, length us, event | category | flops | bytes accessed | tf_op | source)
XLA Modules:
  0.0 418.7 jit_solution(15227816075941876927)
XLA Ops:
  0.6 399.5 %exchange.1 = (f32[6,256,3072]{2,1,0:T(8,128)S(1)}, f32[256,3072]{1,0:T(8,128)S(1)}, f32[4,8,128]{2,1,0:T(8,128)S(1)}, f32[2,256]{1,0:T(2,128)S(1)}, f32[64,3072...) custom-call(bf16[7,256,2048]{2,1,0:T(8,128)(2,1)} %bitcast.8, ...), custom_call_target="tpu_custom_call" | custom-call | tf_op jit(solution)/shard_map/exchange/pallas_call | solution.py:584
  400.1 6.5 %early_output.1 = (f32[6,256,3072]{2,1,0:T(8,128)}, f32[256,3072]{1,0:T(8,128)}, f32[8,128]{1,0:T(8,128)S(1)}) custom-call(f32[6,256,3072]{2,1,0:T(8,128)S(1)} %get-tuple-element.20.ex_ref, f32[256,3072]{1,0:T(8,128)S(1)} %get-tuple-element.26.bonus_ref, f32[4,8,128]{2,1,0:T(8,128)S(1)} %get-tuple-element.27.early_ref), custom_call_target="tpu_custom_call" | custom-call | tf_op jit(solution)/shard_map/early_output/pallas_call | solution.py:603
  406.7 10.1 %last.1 = (f32[64,3072]{1,0:T(8,128)S(1)}, f32[16,2,256]{2,1,0:T(2,128)S(1)}) custom-call(f32[64,3072]{1,0:T(8,128)S(1)} %get-tuple-element.21.q_ref, f32[8,3072]{1,0:T(8,128)S(1)} %get-tuple-element.22.head_ref, f32[64,3072]{1,0:T(8,128)S(1)} %get-tuple-element.23.p_ref, s32[64,128]{1,0:T(8,128)S(1)} %get-tuple-element.24.tok_ref, ...), custom_call_target="tpu_custom_call" | custom-call | tf_op jit(solution)/shard_map/last/pallas_call | solution.py:613
  416.7 1.9 late_output.1

commit v7 on v6

--- a/solution.py
+++ b/solution.py
@@ -161,17 +161,16 @@
     other_planes = [(plane, lax.rem(tb + k, nb)) for plane in (jnp.where(inner, 0, 1), jnp.where(inner, 3, 2)) for k in range(nb)]
 
     barrier = pltpu.get_barrier_semaphore()
-    signal(barrier, partner_plane)
 
     @pl.when(inner)
     def _():
-        signal(barrier, other_planes)
+        signal(barrier, [(partner, tb)] + other_planes)
 
     @pl.when(jnp.logical_not(inner))
     def _():
-        signal(barrier, own_plane)
-
-    pl.semaphore_wait(barrier, jnp.where(inner, nb, n_peers - 1))
+        signal(barrier, partner_plane + own_plane)
+
+    pl.semaphore_wait(barrier, jnp.where(inner, 1, n_peers - 1))
     q_to(0, 0).start()
 
     @pl.when(jnp.logical_not(inner))

time: 419 us -> 418 us (level)
  no operation moved by 1% of the time
where the time goes in v7:
time: 418 us
  Pallas kernels  417 us (100%)
    pallas_call x1, Pallas kernels, local_step(): pl.pallas_call(functools.partial(exchange_kernel, dims), out_shape=(pltpu...  397 us
    pallas_call x1, Pallas kernels, local_step(): pl.pallas_call(functools.partial(last_kernel, (n_draft, seqs, vocab, n_lo...  11.5 us

profile of v7, /device:TPU:0, one launch (start us, length us, event | category | flops | bytes accessed | tf_op | source)
XLA Modules:
  0.0 417.8 jit_solution(16022225736755889515)
XLA Ops:
  0.6 397.3 %exchange.1 = (f32[6,256,3072]{2,1,0:T(8,128)S(1)}, f32[256,3072]{1,0:T(8,128)S(1)}, f32[4,8,128]{2,1,0:T(8,128)S(1)}, f32[2,256]{1,0:T(2,128)S(1)}, f32[64,3072...) custom-call(bf16[7,256,2048]{2,1,0:T(8,128)(2,1)} %bitcast.8, ...), custom_call_target="tpu_custom_call" | custom-call | tf_op jit(solution)/shard_map/exchange/pallas_call | solution.py:583
  397.9 6.5 %early_output.1 = (f32[6,256,3072]{2,1,0:T(8,128)}, f32[256,3072]{1,0:T(8,128)}, f32[8,128]{1,0:T(8,128)S(1)}) custom-call(f32[6,256,3072]{2,1,0:T(8,128)S(1)} %get-tuple-element.20.ex_ref, f32[256,3072]{1,0:T(8,128)S(1)} %get-tuple-element.26.bonus_ref, f32[4,8,128]{2,1,0:T(8,128)S(1)} %get-tuple-element.27.early_ref), custom_call_target="tpu_custom_call" | custom-call | tf_op jit(solution)/shard_map/early_output/pallas_call | solution.py:602
  404.4 11.5 %last.1 = (f32[64,3072]{1,0:T(8,128)S(1)}, f32[16,2,256]{2,1,0:T(2,128)S(1)}) custom-call(f32[64,3072]{1,0:T(8,128)S(1)} %get-tuple-element.21.q_ref, f32[8,3072]{1,0:T(8,128)S(1)} %get-tuple-element.22.head_ref, f32[64,3072]{1,0:T(8,128)S(1)} %get-tuple-element.23.p_ref, s32[64,128]{1,0:T(8,128)S(1)} %get-tuple-element.24.tok_ref, ...), custom_call_target="tpu_custom_call" | custom-call | tf_op jit(solution)/shard_map/last/pallas_call | solution.py:612
  415.9 1.9 late_output.1

commit v8 on v7

--- a/solution.py
+++ b/solution.py
@@ -192,10 +192,6 @@
         for k in range(1, 4):
             q_to(0, k).start()
 
-    x_copy.wait()
-    tok_rows = x_v[...].astype(F32)
-    for i in range(n_draft):
-        tok_v[i] = jnp.broadcast_to(to_col(tok_rows[i:i + 1]), (seqs, 128)).astype(jnp.int32) - me * vocab
     hid_copy.wait()
     for copy in part_copies:
         copy.wait()
@@ -229,18 +225,29 @@
         stat_out[core] = lax.fori_loop(0, na, plane_rows, jnp.zeros((8, 128), F32))
 
     stat_1[tb] = stat_out[tb]
+
+    x_copy.wait()
+    tok_rows = x_v[...].astype(F32)
+
+    def token_columns(positions):
+        for i in positions:
+            tok_v[i] = jnp.broadcast_to(to_col(tok_rows[i:i + 1]), (seqs, 128)).astype(jnp.int32) - me * vocab
+
+    token_columns(range(2))
     start(in_plane(stat_out, stat_1, a1_send, a1_recv, True))
     await_slots(stat_1, a1_recv, 3)
     stat_2[za] = jnp.concatenate(combine(stat_1), axis=0)
+    token_columns(range(2, 4))
     start(across(stat_2, a2_send, a2_recv))
-    for k in (4, 5):
+    for k in (4,):
         q_to(0, k).start()
     await_slots(stat_2, a2_recv, 3)
     top, total = combine(stat_2)
     used = lax.broadcasted_iota(jnp.int32, (4, 128), 1) < n_pos * n_loc
     norm_v[tb] = jnp.concatenate([top, 1.0 / jnp.where(used, total, 1.0)], axis=0)
+    token_columns(range(4, n_draft))
     start(in_plane(norm_v, norm_v, a3_send, a3_recv, False))
-    for k in range(6, 15):
+    for k in range(5, 15):
         q_to(0, k).start()
     for k in range(10):
         q_to(1, k).start()

time: 418 us -> 418 us (level)
  no operation moved by 1% of the time
where the time goes in v8:
time: 418 us
  Pallas kernels  417 us (100%)
    pallas_call x1, Pallas kernels, local_step(): pl.pallas_call(functools.partial(exchange_kernel, dims), out_shape=(pltpu...  397 us
    pallas_call x1, Pallas kernels, local_step(): pl.pallas_call(functools.partial(last_kernel, (n_draft, seqs, vocab, n_lo...  11.3 us

profile of v8, /device:TPU:0, one launch (start us, length us, event | category | flops | bytes accessed | tf_op | source)
XLA Modules:
  0.0 417.7 jit_solution(17215350992671138638)
XLA Ops:
  0.6 397.2 %exchange.1 = (f32[6,256,3072]{2,1,0:T(8,128)S(1)}, f32[256,3072]{1,0:T(8,128)S(1)}, f32[4,8,128]{2,1,0:T(8,128)S(1)}, f32[2,256]{1,0:T(2,128)S(1)}, f32[64,3072...) custom-call(bf16[7,256,2048]{2,1,0:T(8,128)(2,1)} %bitcast.8, ...), custom_call_target="tpu_custom_call" | custom-call | tf_op jit(solution)/shard_map/exchange/pallas_call | solution.py:590
  397.9 6.5 %early_output.1 = (f32[6,256,3072]{2,1,0:T(8,128)}, f32[256,3072]{1,0:T(8,128)}, f32[8,128]{1,0:T(8,128)S(1)}) custom-call(f32[6,256,3072]{2,1,0:T(8,128)S(1)} %get-tuple-element.20.ex_ref, f32[256,3072]{1,0:T(8,128)S(1)} %get-tuple-element.26.bonus_ref, f32[4,8,128]{2,1,0:T(8,128)S(1)} %get-tuple-element.27.early_ref), custom_call_target="tpu_custom_call" | custom-call | tf_op jit(solution)/shard_map/early_output/pallas_call | solution.py:609
  404.4 11.3 %last.1 = (f32[64,3072]{1,0:T(8,128)S(1)}, f32[16,2,256]{2,1,0:T(2,128)S(1)}) custom-call(f32[64,3072]{1,0:T(8,128)S(1)} %get-tuple-element.21.q_ref, f32[8,3072]{1,0:T(8,128)S(1)} %get-tuple-element.22.head_ref, f32[64,3072]{1,0:T(8,128)S(1)} %get-tuple-element.23.p_ref, s32[64,128]{1,0:T(8,128)S(1)} %get-tuple-element.24.tok_ref, ...), custom_call_target="tpu_custom_call" | custom-call | tf_op jit(solution)/shard_map/last/pallas_call | solution.py:619
  415.8 1.9 late_output.1

commit v9 on v8

--- a/solution.py
+++ b/solution.py
@@ -447,12 +447,16 @@
 
     @pl.when(inner)
     def _():
+        pl.semaphore_wait(ready, 2 * nb)
+
+    for peer in other + same:
+        late_to(peer).start()
+
+    @pl.when(inner)
+    def _():
         sent = q_ref.at[pl.ds(0, nb * n_loc - n_loc // 2), :]
         pltpu.make_async_copy(sent, sent, q_send).wait()
-        pl.semaphore_wait(ready, 2 * nb)
-
-    for peer in other + same:
-        late_to(peer).start()
+
     slots = late_ref.at[pl.ds(0, n_peers - 1)]
     pltpu.make_async_copy(slots, slots, l_recv).wait()
     pltpu.make_async_copy(slots, slots, l_send).wait()
@@ -529,29 +533,27 @@
         late += late_ref[k]
     col = to_col(1.0 / late[0:1])
 
-    def out_copy(plane):
-        rows = pl.ds(plane * block, block)
-        return pltpu.make_async_copy(stage.at[rows], res_ref.at[n_early, rows, :], stage_sem.at[plane])
-
-    for plane in range(na):
-        rows, scale = pl.ds(plane * block, block), col[plane * block:(plane + 1) * block]
-        from_part = inner & (partner == plane)
+    pieces = 2 * na
+    rows_each = seqs // pieces
+
+    def out_copy(piece):
+        rows = pl.ds(piece * rows_each, rows_each)
+        return pltpu.make_async_copy(stage.at[rows], res_ref.at[n_early, rows, :], stage_sem.at[piece])
+
+    for piece in range(pieces):
+        first = piece * rows_each
+        rows, scale = pl.ds(first, rows_each), col[first:first + rows_each]
+        from_part = inner & (partner == first // block)
 
         @pl.when(from_part)
         def _():
-            @pl.loop(0, vocab // NT)
-            def _(t):
-                cols = pl.ds(pl.multiple_of(t * NT, NT), NT)
-                stage[rows, cols] = part_ref[:, cols] * scale
+            stage[rows, :] = part_ref[pl.ds(first % block, rows_each), :] * scale
 
         @pl.when(jnp.logical_not(from_part))
         def _():
-            @pl.loop(0, vocab // NT)
-            def _(t):
-                cols = pl.ds(pl.multiple_of(t * NT, NT), NT)
-                stage[rows, cols] = ex_ref[n_early, rows, cols] * scale
-
-        out_copy(plane).start()
+            stage[rows, :] = ex_ref[n_early, rows, :] * scale
+
+        out_copy(piece).start()
 
     accept = by_position(na, nb, early_ref, 1, n_early, seqs)
     accept = jnp.where(lax.broadcasted_iota(jnp.int32, accept.shape, 0) == n_early, late[1:2], accept)[:n_draft]
@@ -566,8 +568,8 @@
                     pltpu.make_async_copy(expected_v, expected_ref, small_sem.at[1]))
     for copy in small_copies:
         copy.start()
-    for plane in range(na):
-        out_copy(plane).wait()
+    for piece in range(pieces):
+        out_copy(piece).wait()
     for copy in small_copies:
         copy.wait()
 
@@ -632,7 +634,7 @@
             in_specs=[vmem_spec] * 4 + [any_spec],
             out_specs=(any_spec,) * 3,
             scratch_shapes=[pltpu.VMEM((seqs, vocab), F32), pltpu.VMEM((n_draft, seqs), F32), pltpu.VMEM((1, seqs), F32),
-                            dma((na,)), dma((2,))],
+                            dma((2 * na,)), dma((2,))],
             input_output_aliases={4: 0},
             compiler_params=pltpu.CompilerParams(vmem_limit_bytes=12 * 2**20),
             name="late_output",

time: 418 us -> 418 us (level)
  no operation moved by 1% of the time
where the time goes in v9:
time: 418 us
  Pallas kernels  417 us (100%)
    pallas_call x1, Pallas kernels, local_step(): pl.pallas_call(functools.partial(exchange_kernel, dims), out_shape=(pltpu...  397 us
    pallas_call x1, Pallas kernels, local_step(): pl.pallas_call(functools.partial(last_kernel, (n_draft, seqs, vocab, n_lo...  11.3 us

profile of v9, /device:TPU:0, one launch (start us, length us, event | category | flops | bytes accessed | tf_op | source)
XLA Modules:
  0.0 417.7 jit_solution(855827530698001515)
XLA Ops:
  0.6 397.2 %exchange.1 = (f32[6,256,3072]{2,1,0:T(8,128)S(1)}, f32[256,3072]{1,0:T(8,128)S(1)}, f32[4,8,128]{2,1,0:T(8,128)S(1)}, f32[2,256]{1,0:T(2,128)S(1)}, f32[64,3072...) custom-call(bf16[7,256,2048]{2,1,0:T(8,128)(2,1)} %bitcast.8, ...), custom_call_target="tpu_custom_call" | custom-call | tf_op jit(solution)/shard_map/exchange/pallas_call | solution.py:592
  397.9 6.5 %early_output.1 = (f32[6,256,3072]{2,1,0:T(8,128)}, f32[256,3072]{1,0:T(8,128)}, f32[8,128]{1,0:T(8,128)S(1)}) custom-call(f32[6,256,3072]{2,1,0:T(8,128)S(1)} %get-tuple-element.20.ex_ref, f32[256,3072]{1,0:T(8,128)S(1)} %get-tuple-element.26.bonus_ref, f32[4,8,128]{2,1,0:T(8,128)S(1)} %get-tuple-element.27.early_ref), custom_call_target="tpu_custom_call" | custom-call | tf_op jit(solution)/shard_map/early_output/pallas_call | solution.py:611
  404.4 11.3 %last.1 = (f32[64,3072]{1,0:T(8,128)S(1)}, f32[16,2,256]{2,1,0:T(2,128)S(1)}) custom-call(f32[64,3072]{1,0:T(8,128)S(1)} %get-tuple-element.21.q_ref, f32[8,3072]{1,0:T(8,128)S(1)} %get-tuple-element.22.head_ref, f32[64,3072]{1,0:T(8,128)S(1)} %get-tuple-element.23.p_ref, s32[64,128]{1,0:T(8,128)S(1)} %get-tuple-element.24.tok_ref, ...), custom_call_target="tpu_custom_call" | custom-call | tf_op jit(solution)/shard_map/last/pallas_call | solution.py:621
  415.8 1.9 late_output.1
